TPU v7x, 32 devices: a whole 2x2x4 slice. The times are simulated.
32 devices in a mesh: section: 8 (over z, core), tm: 4 (over y, x).
Axes of the slice: x: 2, y: 2, z: 4, core: 2. Of those that a mesh axis runs over, the one named last changes fastest.
Arguments:
- frames: bfloat16 [4, 256, 1024], P(None, 'tm'), may hold values from -6 to 6, as said below
- lengths: int32 [4], replicated, may hold values from 64 to 256
- ffn_gain: float32 [8, 1024], P('section'), may hold values from 0.1 to 1.9
- ffn_up: bfloat16 [8, 1024, 2048], P('section'), may hold values from -0.1875 to 0.1875
- ffn_down: bfloat16 [8, 2048, 1024], P('section'), may hold values from -0.125 to 0.125
- attn_gain: float32 [8, 1024], P('section'), may hold values from 0.1 to 1.9
- query_weight: bfloat16 [8, 1024, 1024], P('section'), may hold values from -8 to 8
- key_weight: bfloat16 [8, 1024, 1024], P('section'), may hold values from -0.1875 to 0.1875
- value_weight: bfloat16 [8, 1024, 1024], P('section'), may hold values from -0.1875 to 0.1875
- out_weight: bfloat16 [8, 1024, 1024], P('section'), may hold values from -0.1875 to 0.1875
- conv_gain: float32 [8, 1024], P('section'), may hold values from 0.1 to 1.9
- expand_weight: bfloat16 [8, 1024, 2048], P('section'), may hold values from -0.1875 to 0.1875
- depth_weight: float32 [8, 31, 1024], P('section'), may hold values from -1 to 1
- depth_gain: float32 [8, 1024], P('section'), may hold values from 0.1 to 1.9
- norm_shift: float32 [8, 1024], P('section'), may hold values from -0.5 to 0.5
- shrink_weight: bfloat16 [8, 1024, 1024], P('section'), may hold values from -0.1875 to 0.1875
- final_gain: float32 [8, 1024], P('section'), may hold values from 0.1 to 1.9
Outputs:
- hidden_states: bfloat16 [8, 4, 256, 1024], P('section', None, 'tm')
Inputs may be any that keep to these rules, and one draw needn't show every extreme that they name: `frames`: input features of order one.
All inputs are finite; a program needn't handle non-finite values.
Results may differ from a plain program's by a relative error of at most 0.02.
Values may be sent and summed in bfloat16 or wider, within the bound.
No kernel may reach another device: no remote copies, remote signals or barrier semaphores. Data moves between devices by JAX's collectives and lax.ppermute only.
A program may use at most 128 MiB of HBM per device.

v0:
```python
import math

import jax
import jax.numpy as jnp
from jax import lax
from jax.sharding import PartitionSpec as P

HEADS = 16


EPS = 1e-05


def extended(shard, sides, width):
    for axis, dim in sides:
        peers, length = (lax.axis_size(axis), shard.shape[dim])
        up = [(i, (i + 1) % peers) for i in range(peers - 1)]
        down = [(j, i) for i, j in up]
        last = lax.slice_in_dim(shard, length - width, length, axis=dim)
        initial = lax.slice_in_dim(shard, 0, width, axis=dim)
        before = lax.ppermute(last, axis, up)
        after = lax.ppermute(initial, axis, down)
        shard = jnp.concatenate([before, shard, after], axis=dim)
    return shard


def passed_along(shard, axis, by):
    peers = lax.axis_size(axis)
    pairs = [(i, i + by) for i in range(peers) if 0 <= i + by < peers]
    return lax.ppermute(shard, axis, pairs)


def normalize(value, gain):
    mean = jnp.mean(value, axis=-1, keepdims=True)
    centred = value - mean
    spread = jnp.mean(centred * centred, axis=-1, keepdims=True)
    return centred * lax.rsqrt(spread + EPS) * gain


def body(
    frames,
    lengths,
    ffn_gain,
    ffn_up,
    ffn_down,
    attn_gain,
    query_weight,
    key_weight,
    value_weight,
    out_weight,
    conv_gain,
    expand_weight,
    depth_weight,
    depth_gain,
    norm_shift,
    shrink_weight,
    final_gain,
):
    sections = lax.axis_size("section")
    section_index = lax.axis_index("section")
    group_index = lax.axis_index("tm")
    micro, rows, width = frames.shape
    heads = HEADS
    head = width // heads
    kernel = depth_weight.shape[1]
    rim = kernel // 2
    scale = 1.0 / math.sqrt(head)
    gain_ffn = ffn_gain[0]
    w_up = ffn_up[0]
    w_down = ffn_down[0]
    gain_a = attn_gain[0]
    w_query = query_weight[0]
    w_key = key_weight[0]
    w_value = value_weight[0]
    w_out = out_weight[0]
    gain_c = conv_gain[0]
    w_expand = expand_weight[0]
    w_depth = depth_weight[0]
    gain_depth = depth_gain[0]
    bias_depth = norm_shift[0]
    w_shrink = shrink_weight[0]
    gain_f = final_gain[0]
    local_pos = group_index * rows + jnp.arange(rows, dtype=jnp.int32)
    zero_rows = jnp.zeros((rows, width), jnp.bfloat16)
    zero_mid = jnp.zeros((rows, width), jnp.float32)

    def tick(step, carry):
        incoming, gathered = carry
        offset = step - section_index
        active = (offset >= 0) & (offset < micro)
        slot = jnp.clip(offset, 0, micro - 1)
        fresh = lax.dynamic_index_in_dim(frames, slot, 0, keepdims=False)
        inputs = jnp.where(section_index == 0, fresh, incoming)
        length = jnp.sum(jnp.where(jnp.arange(micro, dtype=jnp.int32) == slot, lengths, 0))

        def project():
            ffn_normed = normalize(inputs.astype(jnp.float32), gain_ffn).astype(jnp.bfloat16)
            inner = jax.nn.silu(
                jnp.dot(ffn_normed, w_up, preferred_element_type=jnp.float32)
            ).astype(jnp.bfloat16)
            start = inputs.astype(jnp.float32) + 0.5 * jnp.dot(
                inner, w_down, preferred_element_type=jnp.float32
            )
            normed = normalize(start, gain_a).astype(jnp.bfloat16)
            q_all, k_all, v_all = tuple(
                (
                    jnp.dot(normed, weight, preferred_element_type=jnp.float32).astype(jnp.bfloat16)
                    for weight in (w_query, w_key, w_value)
                )
            )
            return (start, q_all, k_all, v_all)

        start, queries, keys, values = lax.cond(
            active, project, lambda: (zero_mid, zero_rows, zero_rows, zero_rows)
        )
        q_heads = queries.reshape(rows, heads, head)

        def piece_scores(piece):
            k_piece = piece.reshape(piece.shape[0], heads, head)
            scores = (
                jnp.einsum("qhd,khd->hqk", q_heads, k_piece, preferred_element_type=jnp.float32)
                * scale
            )
            seen = jnp.arange(piece.shape[0], dtype=jnp.int32) < length
            return jnp.where(seen[None, None, :], scores, -1e30)

        best = jnp.full((heads, rows), -1e30, jnp.float32)
        piece = lax.all_gather(keys, "tm", axis=0, tiled=True)
        peak = lax.cond(
            active, lambda: jnp.maximum(best, jnp.max(piece_scores(piece), axis=-1)), lambda: best
        )
        start_sums = (
            jnp.zeros((heads, rows), jnp.float32),
            jnp.zeros((heads, rows, head), jnp.float32),
        )
        pieces = (
            lax.all_gather(keys, "tm", axis=0, tiled=True),
            lax.all_gather(values, "tm", axis=0, tiled=True),
        )

        def grow():
            weights_h = jnp.exp(piece_scores(pieces[0]) - peak[:, :, None])
            v_piece = pieces[1].reshape(pieces[1].shape[0], heads, head)
            mixed = jnp.einsum(
                "hqk,khd->hqd",
                weights_h.astype(jnp.bfloat16),
                v_piece,
                preferred_element_type=jnp.float32,
            )
            return (jnp.sum(weights_h, axis=-1), mixed)

        total, accum = lax.cond(active, grow, lambda: start_sums)
        denom = jnp.where(active, total, 1.0)
        context = (
            jnp.transpose(accum / denom[:, :, None], (1, 0, 2))
            .reshape(rows, width)
            .astype(jnp.bfloat16)
        )

        def conv_front():
            mid = start + jnp.dot(context, w_out, preferred_element_type=jnp.float32)
            conv_in = normalize(mid, gain_c).astype(jnp.bfloat16)
            expanded = jnp.dot(conv_in, w_expand, preferred_element_type=jnp.float32)
            keep = (local_pos < length).astype(jnp.float32)
            glu = expanded[:, :width] * jax.nn.sigmoid(expanded[:, width:]) * keep[:, None]
            return (mid, glu.astype(jnp.bfloat16))

        mid, glu = lax.cond(active, conv_front, lambda: (zero_mid, zero_rows))
        padded = extended(glu, (("tm", 0),), rim)

        def conv_back():
            widened = padded.astype(jnp.float32)
            depth = jnp.zeros((rows, width), jnp.float32)
            for offset_j in range(kernel):
                depth = depth + widened[offset_j : offset_j + rows] * w_depth[offset_j]
            shifted = normalize(depth, gain_depth) + bias_depth
            swished = (shifted * jax.nn.sigmoid(shifted)).astype(jnp.bfloat16)
            closing = mid + jnp.dot(swished, w_shrink, preferred_element_type=jnp.float32)
            return normalize(closing, gain_f).astype(jnp.bfloat16)

        result = lax.cond(active, conv_back, lambda: zero_rows)
        previous = lax.dynamic_index_in_dim(gathered, slot, 0, keepdims=False)
        gathered = lax.dynamic_update_index_in_dim(
            gathered, jnp.where(active, result, previous), slot, 0
        )
        incoming = passed_along(result, "section", 1)
        return (incoming, gathered)

    start_outs = jnp.zeros((micro, rows, width), jnp.bfloat16)
    final_in, hidden_states = lax.fori_loop(0, micro + sections - 1, tick, (zero_rows, start_outs))
    return hidden_states[None]


def solution(mesh):
    return jax.shard_map(
        body,
        mesh=mesh,
        in_specs=(
            P(None, "tm", None),
            P(),
            P("section", None),
            P("section", None, None),
            P("section", None, None),
            P("section", None),
            P("section", None, None),
            P("section", None, None),
            P("section", None, None),
            P("section", None, None),
            P("section", None),
            P("section", None, None),
            P("section", None, None),
            P("section", None),
            P("section", None),
            P("section", None, None),
            P("section", None),
        ),
        out_specs=P("section", None, "tm", None),
        check_vma=False,
    )
```

profile of v0, /device:TPU:25, one launch (start us, length us, event | category | flops | bytes accessed | tf_op | source)
XLA Modules:
  0.0 686.7 jit_solution(15443856810036962053)
XLA Ops:
  2.4 684.3 %while.17 = (s32[]{:T(128)}, bf16[64,1024]{1,0:T(8,128)(2,1)S(1)}, bf16[4,64,1024]{2,1,0:T(8,128)(2,1)}, s32[]{:T(128)}, pred[]{:T(512)}, /*index=5*/bf16[4,64,1...) while((s32[]{:T(128)}, bf16[64,1024]{1,0:T(8,128)(2,1)S(1)}, ...), condition=%wide.region_24.25_spmd.clone, body=%wide.region_0.24_spmd.clone.sunk | while | flops 1588808704 | bytes 95050688 | solution.py:190
  38.9 11.1 %all_gather.21 = bf16[256,1024]{1,0:T(8,128)(2,1)S(1)} all-gather(bf16[64,1024]{1,0:T(8,128)(2,1)S(1)} %get-tuple-element.920), channel_id=1, replica_groups=mesh['section'=8,'tm'=4] {'tm'}, dimensions={0}, use_global_device_ids=true | all-gather | bytes 655360 | tf_op jit(solution)/shard_map/while/body/eval_jaxpr/all_gather | solution.py:137
  68.6 8.7 %collective-permute-done.2 = bf16[64,1024]{1,0:T(8,128)(2,1)S(1)} collective-permute-done((bf16[64,1024]{1,0:T(8,128)(2,1)S(1)}, bf16[64,1024]{1,0:T(8,128)(2,1)S(1)}, u32[]{:S(2)}, u32[]{:S(2)}) %collective-permute-start.2) | collective-permute-done | bytes 131104 | tf_op jit(solution)/shard_map/while/body/eval_jaxpr/ppermute | solution.py:30
  78.8 11.0 %all_gather.21 = bf16[256,1024]{1,0:T(8,128)(2,1)S(1)} all-gather(bf16[64,1024]{1,0:T(8,128)(2,1)S(1)} %get-tuple-element.920), channel_id=1, replica_groups=mesh['section'=8,'tm'=4] {'tm'}, dimensions={0}, use_global_device_ids=true | all-gather | bytes 655360 | tf_op jit(solution)/shard_map/while/body/eval_jaxpr/all_gather | solution.py:137
  108.3 8.7 %collective-permute-done.2 = bf16[64,1024]{1,0:T(8,128)(2,1)S(1)} collective-permute-done((bf16[64,1024]{1,0:T(8,128)(2,1)S(1)}, bf16[64,1024]{1,0:T(8,128)(2,1)S(1)}, u32[]{:S(2)}, u32[]{:S(2)}) %collective-permute-start.2) | collective-permute-done | bytes 131104 | tf_op jit(solution)/shard_map/while/body/eval_jaxpr/ppermute | solution.py:30
  118.5 11.0 %all_gather.21 = bf16[256,1024]{1,0:T(8,128)(2,1)S(1)} all-gather(bf16[64,1024]{1,0:T(8,128)(2,1)S(1)} %get-tuple-element.920), channel_id=1, replica_groups=mesh['section'=8,'tm'=4] {'tm'}, dimensions={0}, use_global_device_ids=true | all-gather | bytes 655360 | tf_op jit(solution)/shard_map/while/body/eval_jaxpr/all_gather | solution.py:137
  148.0 8.7 %collective-permute-done.2 = bf16[64,1024]{1,0:T(8,128)(2,1)S(1)} collective-permute-done((bf16[64,1024]{1,0:T(8,128)(2,1)S(1)}, bf16[64,1024]{1,0:T(8,128)(2,1)S(1)}, u32[]{:S(2)}, u32[]{:S(2)}) %collective-permute-start.2) | collective-permute-done | bytes 131104 | tf_op jit(solution)/shard_map/while/body/eval_jaxpr/ppermute | solution.py:30
  158.2 11.0 %all_gather.21 = bf16[256,1024]{1,0:T(8,128)(2,1)S(1)} all-gather(bf16[64,1024]{1,0:T(8,128)(2,1)S(1)} %get-tuple-element.920), channel_id=1, replica_groups=mesh['section'=8,'tm'=4] {'tm'}, dimensions={0}, use_global_device_ids=true | all-gather | bytes 655360 | tf_op jit(solution)/shard_map/while/body/eval_jaxpr/all_gather | solution.py:137
  187.7 8.7 %collective-permute-done.2 = bf16[64,1024]{1,0:T(8,128)(2,1)S(1)} collective-permute-done((bf16[64,1024]{1,0:T(8,128)(2,1)S(1)}, bf16[64,1024]{1,0:T(8,128)(2,1)S(1)}, u32[]{:S(2)}, u32[]{:S(2)}) %collective-permute-start.2) | collective-permute-done | bytes 131104 | tf_op jit(solution)/shard_map/while/body/eval_jaxpr/ppermute | solution.py:30
  197.9 11.0 %all_gather.21 = bf16[256,1024]{1,0:T(8,128)(2,1)S(1)} all-gather(bf16[64,1024]{1,0:T(8,128)(2,1)S(1)} %get-tuple-element.920), channel_id=1, replica_groups=mesh['section'=8,'tm'=4] {'tm'}, dimensions={0}, use_global_device_ids=true | all-gather | bytes 655360 | tf_op jit(solution)/shard_map/while/body/eval_jaxpr/all_gather | solution.py:137
  227.4 8.7 %collective-permute-done.2 = bf16[64,1024]{1,0:T(8,128)(2,1)S(1)} collective-permute-done((bf16[64,1024]{1,0:T(8,128)(2,1)S(1)}, bf16[64,1024]{1,0:T(8,128)(2,1)S(1)}, u32[]{:S(2)}, u32[]{:S(2)}) %collective-permute-start.2) | collective-permute-done | bytes 131104 | tf_op jit(solution)/shard_map/while/body/eval_jaxpr/ppermute | solution.py:30
  237.5 10.1 %all_gather.21 = bf16[256,1024]{1,0:T(8,128)(2,1)S(1)} all-gather(bf16[64,1024]{1,0:T(8,128)(2,1)S(1)} %get-tuple-element.920), channel_id=1, replica_groups=mesh['section'=8,'tm'=4] {'tm'}, dimensions={0}, use_global_device_ids=true | all-gather | bytes 655360 | tf_op jit(solution)/shard_map/while/body/eval_jaxpr/all_gather | solution.py:137
  265.3 163.8 %collective-permute-done.2 = bf16[64,1024]{1,0:T(8,128)(2,1)S(1)} collective-permute-done((bf16[64,1024]{1,0:T(8,128)(2,1)S(1)}, bf16[64,1024]{1,0:T(8,128)(2,1)S(1)}, u32[]{:S(2)}, u32[]{:S(2)}) %collective-permute-start.2) | collective-permute-done | bytes 131104 | tf_op jit(solution)/shard_map/while/body/eval_jaxpr/ppermute | solution.py:30
  430.4 10.0 %conditional.15 = (f32[64,1024]{1,0:T(8,128)S(1)}, bf16[64,1024]{1,0:T(8,128)(2,1)S(1)}, bf16[64,1024]{1,0:T(8,128)(2,1)S(1)}, bf16[64,16,64]{2,1,0:T(8,128)(2,1)S(1)}) conditional(s32[]{:T(128)} %convert_element_type.123, () %tuple.143, (pred[]{:T(512)}, bf16[4,64,1024]{2,1,0:T(8,128)(2,1)}, s32[]{:T(128)}, bf16[64,1024]{1,0:T(8,128)(2,1)S(1)}, ...), branch_computations={%region_1.1_spmd, %region_2.0_spmd} | conditional | flops 941883520 | bytes 44593868 | solution.py:113
  440.4 12.2 %all_gather.21 = bf16[256,1024]{1,0:T(8,128)(2,1)S(1)} all-gather(bf16[64,1024]{1,0:T(8,128)(2,1)S(1)} %get-tuple-element.920), channel_id=1, replica_groups=mesh['section'=8,'tm'=4] {'tm'}, dimensions={0}, use_global_device_ids=true | all-gather | bytes 655360 | tf_op jit(solution)/shard_map/while/body/eval_jaxpr/all_gather | solution.py:137
  487.4 8.8 %collective-permute-done.2 = bf16[64,1024]{1,0:T(8,128)(2,1)S(1)} collective-permute-done((bf16[64,1024]{1,0:T(8,128)(2,1)S(1)}, bf16[64,1024]{1,0:T(8,128)(2,1)S(1)}, u32[]{:S(2)}, u32[]{:S(2)}) %collective-permute-start.2) | collective-permute-done | bytes 131104 | tf_op jit(solution)/shard_map/while/body/eval_jaxpr/ppermute | solution.py:30
  497.5 10.0 %conditional.15 = (f32[64,1024]{1,0:T(8,128)S(1)}, bf16[64,1024]{1,0:T(8,128)(2,1)S(1)}, bf16[64,1024]{1,0:T(8,128)(2,1)S(1)}, bf16[64,16,64]{2,1,0:T(8,128)(2,1)S(1)}) conditional(s32[]{:T(128)} %convert_element_type.123, () %tuple.143, (pred[]{:T(512)}, bf16[4,64,1024]{2,1,0:T(8,128)(2,1)}, s32[]{:T(128)}, bf16[64,1024]{1,0:T(8,128)(2,1)S(1)}, ...), branch_computations={%region_1.1_spmd, %region_2.0_spmd} | conditional | flops 941883520 | bytes 44593868 | solution.py:113
  507.5 11.5 %all_gather.21 = bf16[256,1024]{1,0:T(8,128)(2,1)S(1)} all-gather(bf16[64,1024]{1,0:T(8,128)(2,1)S(1)} %get-tuple-element.920), channel_id=1, replica_groups=mesh['section'=8,'tm'=4] {'tm'}, dimensions={0}, use_global_device_ids=true | all-gather | bytes 655360 | tf_op jit(solution)/shard_map/while/body/eval_jaxpr/all_gather | solution.py:137
  553.9 8.7 %collective-permute-done.2 = bf16[64,1024]{1,0:T(8,128)(2,1)S(1)} collective-permute-done((bf16[64,1024]{1,0:T(8,128)(2,1)S(1)}, bf16[64,1024]{1,0:T(8,128)(2,1)S(1)}, u32[]{:S(2)}, u32[]{:S(2)}) %collective-permute-start.2) | collective-permute-done | bytes 131104 | tf_op jit(solution)/shard_map/while/body/eval_jaxpr/ppermute | solution.py:30
  564.0 10.0 %conditional.15 = (f32[64,1024]{1,0:T(8,128)S(1)}, bf16[64,1024]{1,0:T(8,128)(2,1)S(1)}, bf16[64,1024]{1,0:T(8,128)(2,1)S(1)}, bf16[64,16,64]{2,1,0:T(8,128)(2,1)S(1)}) conditional(s32[]{:T(128)} %convert_element_type.123, () %tuple.143, (pred[]{:T(512)}, bf16[4,64,1024]{2,1,0:T(8,128)(2,1)}, s32[]{:T(128)}, bf16[64,1024]{1,0:T(8,128)(2,1)S(1)}, ...), branch_computations={%region_1.1_spmd, %region_2.0_spmd} | conditional | flops 941883520 | bytes 44593868 | solution.py:113
  574.0 11.0 %all_gather.21 = bf16[256,1024]{1,0:T(8,128)(2,1)S(1)} all-gather(bf16[64,1024]{1,0:T(8,128)(2,1)S(1)} %get-tuple-element.920), channel_id=1, replica_groups=mesh['section'=8,'tm'=4] {'tm'}, dimensions={0}, use_global_device_ids=true | all-gather | bytes 655360 | tf_op jit(solution)/shard_map/while/body/eval_jaxpr/all_gather | solution.py:137
  619.8 8.7 %collective-permute-done.2 = bf16[64,1024]{1,0:T(8,128)(2,1)S(1)} collective-permute-done((bf16[64,1024]{1,0:T(8,128)(2,1)S(1)}, bf16[64,1024]{1,0:T(8,128)(2,1)S(1)}, u32[]{:S(2)}, u32[]{:S(2)}) %collective-permute-start.2) | collective-permute-done | bytes 131104 | tf_op jit(solution)/shard_map/while/body/eval_jaxpr/ppermute | solution.py:30
  629.9 10.0 %conditional.15 = (f32[64,1024]{1,0:T(8,128)S(1)}, bf16[64,1024]{1,0:T(8,128)(2,1)S(1)}, bf16[64,1024]{1,0:T(8,128)(2,1)S(1)}, bf16[64,16,64]{2,1,0:T(8,128)(2,1)S(1)}) conditional(s32[]{:T(128)} %convert_element_type.123, () %tuple.143, (pred[]{:T(512)}, bf16[4,64,1024]{2,1,0:T(8,128)(2,1)}, s32[]{:T(128)}, bf16[64,1024]{1,0:T(8,128)(2,1)S(1)}, ...), branch_computations={%region_1.1_spmd, %region_2.0_spmd} | conditional | flops 941883520 | bytes 44593868 | solution.py:113
  639.9 10.1 %all_gather.21 = bf16[256,1024]{1,0:T(8,128)(2,1)S(1)} all-gather(bf16[64,1024]{1,0:T(8,128)(2,1)S(1)} %get-tuple-element.920), channel_id=1, replica_groups=mesh['section'=8,'tm'=4] {'tm'}, dimensions={0}, use_global_device_ids=true | all-gather | bytes 655360 | tf_op jit(solution)/shard_map/while/body/eval_jaxpr/all_gather | solution.py:137
  (674 shorter events, 419.2 us)
Async XLA Ops:
  23.0 6.2 collective-permute-start
  29.4 8.0 %collective-permute-start.2 = (bf16[64,1024]{1,0:T(8,128)(2,1)S(1)}, bf16[64,1024]{1,0:T(8,128)(2,1)S(1)}, u32[]{:S(2)}, u32[]{:S(2)}) collective-permute-start(bf16[64,1024]{1,0:T(8,128)(2,1)S(1)} %get-tuple-element.1028), channel_id=1, source_target_pairs={{0,4},{4,8},{8,12},{12,16},{16,20},{20,24},{24,28},{1,5},{5,9},{9,... | collective-permute-start | bytes 393224 | tf_op jit(solution)/shard_map/while/body/eval_jaxpr/ppermute | solution.py:30
  60.2 6.2 collective-permute-start
  61.5 5.0 collective-permute-start.1
  66.6 10.7 %collective-permute-start.2 = (bf16[64,1024]{1,0:T(8,128)(2,1)S(1)}, bf16[64,1024]{1,0:T(8,128)(2,1)S(1)}, u32[]{:S(2)}, u32[]{:S(2)}) collective-permute-start(bf16[64,1024]{1,0:T(8,128)(2,1)S(1)} %get-tuple-element.1028), channel_id=1, source_target_pairs={{0,4},{4,8},{8,12},{12,16},{16,20},{20,24},{24,28},{1,5},{5,9},{9,... | collective-permute-start | bytes 393224 | tf_op jit(solution)/shard_map/while/body/eval_jaxpr/ppermute | solution.py:30
  99.9 6.2 collective-permute-start
  101.2 5.0 collective-permute-start.1
  106.3 10.7 %collective-permute-start.2 = (bf16[64,1024]{1,0:T(8,128)(2,1)S(1)}, bf16[64,1024]{1,0:T(8,128)(2,1)S(1)}, u32[]{:S(2)}, u32[]{:S(2)}) collective-permute-start(bf16[64,1024]{1,0:T(8,128)(2,1)S(1)} %get-tuple-element.1028), channel_id=1, source_target_pairs={{0,4},{4,8},{8,12},{12,16},{16,20},{20,24},{24,28},{1,5},{5,9},{9,... | collective-permute-start | bytes 393224 | tf_op jit(solution)/shard_map/while/body/eval_jaxpr/ppermute | solution.py:30
  139.6 6.2 collective-permute-start
  146.0 10.7 %collective-permute-start.2 = (bf16[64,1024]{1,0:T(8,128)(2,1)S(1)}, bf16[64,1024]{1,0:T(8,128)(2,1)S(1)}, u32[]{:S(2)}, u32[]{:S(2)}) collective-permute-start(bf16[64,1024]{1,0:T(8,128)(2,1)S(1)} %get-tuple-element.1028), channel_id=1, source_target_pairs={{0,4},{4,8},{8,12},{12,16},{16,20},{20,24},{24,28},{1,5},{5,9},{9,... | collective-permute-start | bytes 393224 | tf_op jit(solution)/shard_map/while/body/eval_jaxpr/ppermute | solution.py:30
  179.2 6.2 collective-permute-start
  185.7 10.7 %collective-permute-start.2 = (bf16[64,1024]{1,0:T(8,128)(2,1)S(1)}, bf16[64,1024]{1,0:T(8,128)(2,1)S(1)}, u32[]{:S(2)}, u32[]{:S(2)}) collective-permute-start(bf16[64,1024]{1,0:T(8,128)(2,1)S(1)} %get-tuple-element.1028), channel_id=1, source_target_pairs={{0,4},{4,8},{8,12},{12,16},{16,20},{20,24},{24,28},{1,5},{5,9},{9,... | collective-permute-start | bytes 393224 | tf_op jit(solution)/shard_map/while/body/eval_jaxpr/ppermute | solution.py:30
  218.9 6.2 collective-permute-start
  225.4 10.7 %collective-permute-start.2 = (bf16[64,1024]{1,0:T(8,128)(2,1)S(1)}, bf16[64,1024]{1,0:T(8,128)(2,1)S(1)}, u32[]{:S(2)}, u32[]{:S(2)}) collective-permute-start(bf16[64,1024]{1,0:T(8,128)(2,1)S(1)} %get-tuple-element.1028), channel_id=1, source_target_pairs={{0,4},{4,8},{8,12},{12,16},{16,20},{20,24},{24,28},{1,5},{5,9},{9,... | collective-permute-start | bytes 393224 | tf_op jit(solution)/shard_map/while/body/eval_jaxpr/ppermute | solution.py:30
  256.8 6.2 collective-permute-start
  258.1 5.0 collective-permute-start.1
  263.3 165.8 %collective-permute-start.2 = (bf16[64,1024]{1,0:T(8,128)(2,1)S(1)}, bf16[64,1024]{1,0:T(8,128)(2,1)S(1)}, u32[]{:S(2)}, u32[]{:S(2)}) collective-permute-start(bf16[64,1024]{1,0:T(8,128)(2,1)S(1)} %get-tuple-element.1028), channel_id=1, source_target_pairs={{0,4},{4,8},{8,12},{12,16},{16,20},{20,24},{24,28},{1,5},{5,9},{9,... | collective-permute-start | bytes 393224 | tf_op jit(solution)/shard_map/while/body/eval_jaxpr/ppermute | solution.py:30
  475.3 6.2 collective-permute-start
  485.4 10.8 %collective-permute-start.2 = (bf16[64,1024]{1,0:T(8,128)(2,1)S(1)}, bf16[64,1024]{1,0:T(8,128)(2,1)S(1)}, u32[]{:S(2)}, u32[]{:S(2)}) collective-permute-start(bf16[64,1024]{1,0:T(8,128)(2,1)S(1)} %get-tuple-element.1028), channel_id=1, source_target_pairs={{0,4},{4,8},{8,12},{12,16},{16,20},{20,24},{24,28},{1,5},{5,9},{9,... | collective-permute-start | bytes 393224 | tf_op jit(solution)/shard_map/while/body/eval_jaxpr/ppermute | solution.py:30
  541.8 6.2 collective-permute-start
  551.9 10.7 %collective-permute-start.2 = (bf16[64,1024]{1,0:T(8,128)(2,1)S(1)}, bf16[64,1024]{1,0:T(8,128)(2,1)S(1)}, u32[]{:S(2)}, u32[]{:S(2)}) collective-permute-start(bf16[64,1024]{1,0:T(8,128)(2,1)S(1)} %get-tuple-element.1028), channel_id=1, source_target_pairs={{0,4},{4,8},{8,12},{12,16},{16,20},{20,24},{24,28},{1,5},{5,9},{9,... | collective-permute-start | bytes 393224 | tf_op jit(solution)/shard_map/while/body/eval_jaxpr/ppermute | solution.py:30
  607.7 6.2 collective-permute-start
  617.8 10.7 %collective-permute-start.2 = (bf16[64,1024]{1,0:T(8,128)(2,1)S(1)}, bf16[64,1024]{1,0:T(8,128)(2,1)S(1)}, u32[]{:S(2)}, u32[]{:S(2)}) collective-permute-start(bf16[64,1024]{1,0:T(8,128)(2,1)S(1)} %get-tuple-element.1028), channel_id=1, source_target_pairs={{0,4},{4,8},{8,12},{12,16},{16,20},{20,24},{24,28},{1,5},{5,9},{9,... | collective-permute-start | bytes 393224 | tf_op jit(solution)/shard_map/while/body/eval_jaxpr/ppermute | solution.py:30
  673.4 6.2 collective-permute-start
  (114 other events, 721.2 us)
where the time goes:
time: 691 us; the launch traced here: 687 us
  waiting for transfers between devices  242 us (35%)
  blocking collectives  203 us (29%)
  starting transfers between devices  72.3 us (10%)
  matrix products  71.3 us (10%)
  other arithmetic  49.6 us (7%)
  local copies, waits for them, and re-layouts  44.5 us (6%)
    ppermute x11, waiting for transfers between devices, passed_along(): return lax.ppermute(shard, axis, pairs)  241 us
    all_gather x11, blocking collectives, tick(): lax.all_gather(keys, 'tm', axis=0, tiled=True)  118 us
    all_gather x11, blocking collectives, tick(): lax.all_gather(values, 'tm', axis=0, tiled=True)  85.5 us
    ppermute x11, starting transfers between devices, extended(): before = lax.ppermute(last, axis, up)  43.9 us
    dot_general x4, matrix products, project(): jnp.dot(inner, w_down, preferred_element_type=jnp.float32)  21.4 us
    reduce_sum x11, other arithmetic, tick(): jnp.sum(jnp.where(jnp.arange(micro, dtype=jnp.int32) == slot, lengths, 0))  14.5 us
    dot_general x8, matrix products, piece_scores(): jnp.einsum('qhd,khd->hqk', q_heads, k_piece, preferred_element_type=jnp.f...  14.5 us
    ppermute x11, starting transfers between devices, passed_along(): return lax.ppermute(shard, axis, pairs)  14.2 us
  transfers between devices with their start and end apart: 33, of which 22 were waited for; matrix products, arithmetic and copies ran while one was open for 3% of the time, Pallas kernels for 0%

commit v1 on v0

v1 whole, which is shorter than its diff:
```python
import math

import jax
import jax.numpy as jnp
from jax import lax
from jax.experimental import pallas as pl
from jax.experimental.pallas import tpu as pltpu
from jax.sharding import PartitionSpec as P

HEADS = 16
EPS = 1e-05
LANES = 128
F32 = jnp.float32
BF16 = jnp.bfloat16


def sigmoid(value):
    return 0.5 * jnp.tanh(0.5 * value) + 0.5


def normalize(value, gain):
    mean = jnp.mean(value, axis=-1, keepdims=True)
    centred = value - mean
    spread = jnp.mean(centred * centred, axis=-1, keepdims=True)
    return centred * lax.rsqrt(spread + EPS) * gain


def dot(left, right):
    return jnp.dot(left, right, preferred_element_type=F32)


def block_kernel(heads, kernel, cols):
    def run(
        info,
        inputs,
        small,
        up,
        down,
        query,
        key,
        value,
        out,
        expand,
        shrink,
        kept,
        result,
        x_s,
        small_s,
        up_s,
        down_s,
        query_s,
        key_s,
        value_s,
        out_s,
        expand_s,
        shrink_s,
        norm_s,
        inner_s,
        start_s,
        q_s,
        k_s,
        v_s,
        glu_s,
        depth_s,
        sems,
    ):
        length, width = x_s.shape
        hidden = inner_s.shape[1]
        head = width // heads
        rim = kernel // 2
        pad = (glu_s.shape[0] - length) // 2

        @pl.when(info[0] == 1)
        def active():
            copies = []

            def fetch(source, target):
                copy = pltpu.make_async_copy(source, target, sems.at[len(copies)])
                copy.start()
                copies.append(copy)
                return copy

            get_x = fetch(inputs, x_s)
            get_small = fetch(small, small_s)
            get_up = [
                fetch(up.at[0, :, pl.ds(j, cols)], up_s.at[:, pl.ds(j, cols)])
                for j in range(0, hidden, cols)
            ]
            get_down = fetch(down.at[0], down_s)
            get_query = fetch(query.at[0], query_s)
            get_key = fetch(key.at[0], key_s)
            get_value = fetch(value.at[0], value_s)
            get_out = fetch(out.at[0], out_s)
            get_expand = fetch(expand.at[0], expand_s)
            get_shrink = fetch(shrink.at[0], shrink_s)

            step = 32

            def rows_loop(fn):
                def one(i, carry):
                    fn(pl.ds(pl.multiple_of(i * step, step), step))
                    return carry

                lax.fori_loop(0, length // step, one, 0, unroll=2)

            zero = jnp.zeros((pad, width), F32)
            glu_s[0:pad, :] = zero
            glu_s[pad + length : pad + length + pad, :] = zero

            get_x.wait()
            get_small.wait()

            def ffn_norm(at):
                norm_s[at, :] = normalize(x_s[at, :].astype(F32), small_s[0:1, :]).astype(BF16)

            rows_loop(ffn_norm)
            for index, j in enumerate(range(0, hidden, cols)):
                get_up[index].wait()
                part = dot(norm_s[...], up_s[:, j : j + cols])
                inner_s[:, j : j + cols] = (part * sigmoid(part)).astype(BF16)
            get_down.wait()
            for j in range(0, width, cols):
                part = dot(inner_s[...], down_s[:, j : j + cols])
                start_s[:, j : j + cols] = x_s[:, j : j + cols].astype(F32) + 0.5 * part

            def attn_norm(at):
                norm_s[at, :] = normalize(start_s[at, :], small_s[1:2, :]).astype(BF16)

            rows_loop(attn_norm)
            for get, weight, target in (
                (get_query, query_s, q_s),
                (get_key, key_s, k_s),
                (get_value, value_s, v_s),
            ):
                get.wait()
                for j in range(0, width, cols):
                    target[:, j : j + cols] = dot(norm_s[...], weight[:, j : j + cols]).astype(BF16)

            frames = info[1]
            seen = lax.broadcasted_iota(jnp.int32, (1, length), 1) < frames
            lane = lax.broadcasted_iota(jnp.int32, (1, LANES), 1)
            group = LANES // head
            scale = 1.0 / math.sqrt(head)

            def one_group(g, carry):
                at = pl.ds(pl.multiple_of(g * LANES, LANES), LANES)
                queries, keys, values = q_s[:, at], k_s[:, at], v_s[:, at]
                mixed = jnp.zeros((length, 2 * LANES), F32)
                for h in range(group):
                    mine = (lane >= h * head) & (lane < (h + 1) * head)
                    k_head = jnp.where(mine, keys, jnp.zeros_like(keys))
                    scores = lax.dot_general(
                        queries, k_head, (((1,), (1,)), ((), ())), preferred_element_type=F32
                    )
                    scores = jnp.where(seen, scores * scale, -1e30)
                    peak = jnp.max(scores, axis=-1, keepdims=True)
                    weights = jnp.exp(scores - peak).astype(BF16)
                    v_head = jnp.where(mine, values, jnp.zeros_like(values))
                    ones = jnp.broadcast_to(jnp.where(mine, 1.0, 0.0).astype(BF16), (length, LANES))
                    mixed = mixed + dot(weights, jnp.concatenate([v_head, ones], axis=1))
                norm_s[:, at] = (
                    mixed[:, :LANES] * pl.reciprocal(mixed[:, LANES:], approx=False)
                ).astype(BF16)
                return carry

            lax.fori_loop(0, width // LANES, one_group, 0)

            get_out.wait()
            for j in range(0, width, cols):
                part = dot(norm_s[...], out_s[:, j : j + cols])
                start_s[:, j : j + cols] = start_s[:, j : j + cols] + part

            def conv_norm(at):
                norm_s[at, :] = normalize(start_s[at, :], small_s[2:3, :]).astype(BF16)

            rows_loop(conv_norm)
            get_expand.wait()
            keep = lax.broadcasted_iota(jnp.int32, (length, 1), 0) < frames
            for j in range(0, width, cols // 2):
                part = dot(norm_s[...], expand_s[:, j : j + cols // 2])
                gate = dot(norm_s[...], expand_s[:, width + j : width + j + cols // 2])
                glu = jnp.where(keep, part * sigmoid(gate), 0.0)
                glu_s[pad : pad + length, j : j + cols // 2] = glu.astype(BF16).astype(F32)

            rows = 64
            shift = pad - rim

            def conv(i, carry):
                at = pl.ds(pl.multiple_of((i % (width // LANES)) * LANES, LANES), LANES)
                begin = pl.multiple_of((i // (width // LANES)) * rows, rows)
                wide = glu_s[pl.ds(begin, rows + 2 * pad), at]
                total = jnp.zeros((rows, LANES), F32)
                for r in range(8):
                    taps = [o for o in range(shift, shift + kernel) if o % 8 == r]
                    extent = rows + 8 if r else rows
                    partial = None
                    for o in taps:
                        tap = small_s[pl.ds(6 + o - shift, 1), at]
                        term = wide[o - r : o - r + extent] * tap
                        partial = term if partial is None else partial + term
                    if r:
                        partial = pltpu.roll(partial, extent - r, 0)[:rows]
                    total = total + partial
                depth_s[pl.ds(begin, rows), at] = total
                return carry

            lax.fori_loop(0, (width // LANES) * (length // rows), conv, 0)

            def swish(at):
                shifted = normalize(depth_s[at, :], small_s[3:4, :]) + small_s[4:5, :]
                norm_s[at, :] = (shifted * sigmoid(shifted)).astype(BF16)

            rows_loop(swish)
            get_shrink.wait()
            for j in range(0, width, cols):
                part = dot(norm_s[...], shrink_s[:, j : j + cols])
                start_s[:, j : j + cols] = start_s[:, j : j + cols] + part

            def closing(at):
                x_s[at, :] = normalize(start_s[at, :], small_s[5:6, :]).astype(BF16)

            rows_loop(closing)
            put = pltpu.make_async_copy(x_s, result, sems.at[len(copies)])
            put.start()
            put.wait()

    return run


def block(info, inputs, small, weights, kept, heads, kernel):
    length, width = inputs.shape
    hidden = weights[0].shape[2]
    cols = 512
    pad = 8 * ((kernel // 2 + 8) // 8)
    vmem = [
        ((length, width), BF16),
        (small.shape, F32),
        *((w.shape[1:], BF16) for w in weights),
        ((length, width), BF16),
        ((length, hidden), BF16),
        ((length, width), F32),
        ((length, width), BF16),
        ((length, width), BF16),
        ((length, width), BF16),
        ((length + 2 * pad, width), F32),
        ((length, width), F32),
    ]
    anywhere = pl.BlockSpec(memory_space=pl.ANY)
    return pl.pallas_call(
        block_kernel(heads, kernel, cols),
        out_shape=jax.ShapeDtypeStruct((length, width), BF16),
        in_specs=[pl.BlockSpec(memory_space=pltpu.SMEM)] + [anywhere] * (3 + len(weights)),
        out_specs=anywhere,
        scratch_shapes=[pltpu.VMEM(shape, kind) for shape, kind in vmem]
        + [pltpu.SemaphoreType.DMA((len(weights) + 2 + hidden // cols,))],
        input_output_aliases={3 + len(weights): 0},
        compiler_params=pltpu.CompilerParams(vmem_limit_bytes=60 * 1024 * 1024),
        name="block",
    )(info, inputs, small, *weights, kept)


def body(
    frames,
    lengths,
    ffn_gain,
    ffn_up,
    ffn_down,
    attn_gain,
    query_weight,
    key_weight,
    value_weight,
    out_weight,
    conv_gain,
    expand_weight,
    depth_weight,
    depth_gain,
    norm_shift,
    shrink_weight,
    final_gain,
):
    sections = lax.axis_size("section")
    section_index = lax.axis_index("section")
    group_index = lax.axis_index("tm")
    micro, rows, width = frames.shape
    peers = lax.axis_size("tm")
    share = peers // micro
    assert share * micro == peers
    utterance = group_index // share
    kernel = depth_weight.shape[1]
    weights = (
        ffn_up,
        ffn_down,
        query_weight,
        key_weight,
        value_weight,
        out_weight,
        expand_weight,
        shrink_weight,
    )
    small = jnp.concatenate(
        [ffn_gain, attn_gain, conv_gain, depth_gain, norm_shift, final_gain, depth_weight[0]]
    )
    small = jnp.pad(small, ((0, -small.shape[0] % 8), (0, 0)))
    length = jnp.sum(jnp.where(jnp.arange(micro, dtype=jnp.int32) == utterance, lengths, 0))
    pairs = [(i, i + 1) for i in range(sections - 1)]

    def apply(step, inputs, kept):
        info = jnp.stack([(step == section_index).astype(jnp.int32), length])
        return block(info, inputs, small, weights, kept, HEADS, kernel)

    across = [[u * share + r for u in range(micro)] for r in range(share)] if share > 1 else None
    within = [[u * share + r for r in range(share)] for u in range(micro)]

    def exchange(parts):
        return lax.all_to_all(parts, "tm", 0, 0, axis_index_groups=across, tiled=True)

    own = exchange(frames)
    if share > 1:
        own = lax.all_gather(own, "tm", axis=1, axis_index_groups=within)
    own = own.reshape(micro * share * rows, width)
    kept = apply(0, own, jnp.zeros_like(own))

    def tick(step, kept):
        return apply(step, lax.ppermute(kept, "section", pairs), kept)

    kept = lax.fori_loop(1, sections, tick, kept)
    parts = kept.reshape(micro, share, rows, width)
    if share > 1:
        parts = lax.dynamic_slice_in_dim(parts, group_index % share, 1, 1)
    return exchange(parts[:, 0])[None]


def solution(mesh):
    return jax.shard_map(
        body,
        mesh=mesh,
        in_specs=(
            P(None, "tm", None),
            P(),
            P("section", None),
            P("section", None, None),
            P("section", None, None),
            P("section", None),
            P("section", None, None),
            P("section", None, None),
            P("section", None, None),
            P("section", None, None),
            P("section", None),
            P("section", None, None),
            P("section", None, None),
            P("section", None),
            P("section", None),
            P("section", None, None),
            P("section", None),
        ),
        out_specs=P("section", None, "tm", None),
        check_vma=False,
    )
```

time: 691 us -> 247 us (0.36)
  blocking collectives: 203 us -> 8.38 us
  matrix products: 71.3 us -> 0 us
  waiting for transfers between devices: 242 us -> 177 us
  starting transfers between devices: 72.3 us -> 12.6 us
  other arithmetic: 49.6 us -> 10.4 us
  local copies, waits for them, and re-layouts: 44.5 us -> 9.08 us
  Pallas kernels: 0 us -> 27.9 us
    all_gather x22 -> x0, blocking collectives: 203 us -> none  [the longest x11 118 us: tick(): lax.all_gather(keys, 'tm', axis=0, tiled=True)]
    dot_general x40 -> x0, matrix products: 71.3 us -> none  [the longest x4 21.4 us: project(): jnp.dot(inner, w_down, preferred_element_type=jnp.float32)]
    ppermute x33 -> x7, waiting for transfers between devices: 242 us -> 175 us  [tick(): return apply(step, lax.ppermute(kept, 'section', pairs), kept)]
    ppermute x33 -> x7, starting transfers between devices: 72.3 us -> 9.04 us  [tick(): return apply(step, lax.ppermute(kept, 'section', pairs), kept)]
    reduce_sum x39 -> x1, other arithmetic: 29.7 us -> 1.29 us  [body(): jnp.sum(jnp.where(jnp.arange(micro, dtype=jnp.int32) == utterance, length...]
    pallas_call x0 -> x8, Pallas kernels: none -> 27.9 us  [block(): pl.pallas_call(block_kernel(heads, kernel, cols), out_shape=jax.ShapeDtyp...]
    dynamic_slice x11 -> x0, local copies, waits for them, and re-layouts: 10.1 us -> none  [tick(): previous = lax.dynamic_index_in_dim(gathered, slot, 0, keepdims=False)]
    another operation x0 -> x8, other arithmetic: none -> 9.09 us  [apply(): info = jnp.stack([(step == section_index).astype(jnp.int32), length])]
  transfers between devices with their start and end apart: 33 -> 8, of which waited for: 22 -> 8; matrix products, arithmetic and copies ran while one was open for 3% -> 5% of each run, Pallas kernels for 0% -> 0%
where the time goes in v1:
time: 247 us; the launch traced here: 246 us
  waiting for transfers between devices  177 us (72%)
  Pallas kernels  27.9 us (11%)
  starting transfers between devices  12.6 us (5%)
  other arithmetic  10.4 us (4%)
  local copies, waits for them, and re-layouts  9.08 us (4%)
  blocking collectives  8.38 us (3%)
    ppermute x7, waiting for transfers between devices, tick(): return apply(step, lax.ppermute(kept, 'section', pairs), kept)  175 us
    pallas_call x8, Pallas kernels, block(): pl.pallas_call(block_kernel(heads, kernel, cols), out_shape=jax.ShapeDtyp...  27.9 us
    another operation x8, other arithmetic, apply(): info = jnp.stack([(step == section_index).astype(jnp.int32), length])  9.09 us
    ppermute x7, starting transfers between devices, tick(): return apply(step, lax.ppermute(kept, 'section', pairs), kept)  9.04 us
    all_to_all x1, blocking collectives, exchange(): lax.all_to_all(parts, 'tm', 0, 0, axis_index_groups=across, tiled=True)  8.38 us
    while x14, local copies, waits for them, and re-layouts  5.55 us
  transfers between devices with their start and end apart: 8, of which 8 were waited for; matrix products, arithmetic and copies ran while one was open for 5% of the time, Pallas kernels for 0%

profile of v1, /device:TPU:25, one launch (start us, length us, event | category | flops | bytes accessed | tf_op | source)
XLA Modules:
  0.0 246.1 jit_solution(7730192020837617743)
XLA Ops:
  0.0 3.6 %all-to-all-start = ((bf16[4,64,1024]{2,1,0:T(8,128)(2,1)}), bf16[4,64,1024]{2,1,0:T(8,128)(2,1)S(1)}, u32[]{:S(2)}, u32[]{:S(2)}) async-start(bf16[4,64,1024]{2,1,0:T(8,128)(2,1)} %param.19), calls=%async_computation | async-start | bytes 1048576 | tf_op jit(solution)/shard_map/all_to_all | solution.py:315
  5.6 1.3 fusion
  8.0 2.8 %all-to-all-done = bf16[4,64,1024]{2,1,0:T(8,128)(2,1)S(1)} async-done(((bf16[4,64,1024]{2,1,0:T(8,128)(2,1)}), bf16[4,64,1024]{2,1,0:T(8,128)(2,1)S(1)}, u32[]{:S(2)}, u32[]{:S(2)}) %all-to-all-start) | async-done | bytes 524320 | tf_op jit(solution)/shard_map/all_to_all | solution.py:315
  12.6 224.3 %while.13 = (s32[]{:T(128)}, bf16[256,1024]{1,0:T(8,128)(2,1)S(1)}, s32[]{:T(128)}, s32[]{:T(128)}, f32[40,1024]{1,0:T(8,128)S(1)}, /*index=5*/bf16[1,1024,2048]...) while((s32[]{:T(128)}, bf16[256,1024]{1,0:T(8,128)(2,1)S(1)}, ...), condition=%wide.region_2.3_spmd, body=%wide.region_1.2_spmd.sunk | while | flops 6 | bytes 4194535 | solution.py:326
  12.6 1.3 collective-permute-start
  15.0 2.6 %collective-permute-done.inputs = bf16[256,1024]{1,0:T(8,128)(2,1)S(1)} collective-permute-done((bf16[256,1024]{1,0:T(8,128)(2,1)S(1)}, bf16[256,1024]{1,0:T(8,128)(2,1)S(1)}, u32[]{:S(2)}, u32[]{:S(2)}) %collective-permute-start) | collective-permute-done | bytes 524320 | tf_op jit(solution)/shard_map/while/body/eval_jaxpr/ppermute | solution.py:324
  19.3 1.3 collective-permute-start
  20.6 1.1 pad_add_fusion.3.info
  21.7 8.1 %collective-permute-done.inputs = bf16[256,1024]{1,0:T(8,128)(2,1)S(1)} collective-permute-done((bf16[256,1024]{1,0:T(8,128)(2,1)S(1)}, bf16[256,1024]{1,0:T(8,128)(2,1)S(1)}, u32[]{:S(2)}, u32[]{:S(2)}) %collective-permute-start) | collective-permute-done | bytes 524320 | tf_op jit(solution)/shard_map/while/body/eval_jaxpr/ppermute | solution.py:324
  31.4 1.3 collective-permute-start
  32.7 1.1 pad_add_fusion.3.info
  33.8 8.1 %collective-permute-done.inputs = bf16[256,1024]{1,0:T(8,128)(2,1)S(1)} collective-permute-done((bf16[256,1024]{1,0:T(8,128)(2,1)S(1)}, bf16[256,1024]{1,0:T(8,128)(2,1)S(1)}, u32[]{:S(2)}, u32[]{:S(2)}) %collective-permute-start) | collective-permute-done | bytes 524320 | tf_op jit(solution)/shard_map/while/body/eval_jaxpr/ppermute | solution.py:324
  43.5 1.3 collective-permute-start
  44.8 1.1 pad_add_fusion.3.info
  45.9 8.1 %collective-permute-done.inputs = bf16[256,1024]{1,0:T(8,128)(2,1)S(1)} collective-permute-done((bf16[256,1024]{1,0:T(8,128)(2,1)S(1)}, bf16[256,1024]{1,0:T(8,128)(2,1)S(1)}, u32[]{:S(2)}, u32[]{:S(2)}) %collective-permute-start) | collective-permute-done | bytes 524320 | tf_op jit(solution)/shard_map/while/body/eval_jaxpr/ppermute | solution.py:324
  55.6 1.3 collective-permute-start
  58.0 8.1 %collective-permute-done.inputs = bf16[256,1024]{1,0:T(8,128)(2,1)S(1)} collective-permute-done((bf16[256,1024]{1,0:T(8,128)(2,1)S(1)}, bf16[256,1024]{1,0:T(8,128)(2,1)S(1)}, u32[]{:S(2)}, u32[]{:S(2)}) %collective-permute-start) | collective-permute-done | bytes 524320 | tf_op jit(solution)/shard_map/while/body/eval_jaxpr/ppermute | solution.py:324
  67.7 1.3 collective-permute-start
  69.0 1.1 pad_add_fusion.3.info
  70.1 8.1 %collective-permute-done.inputs = bf16[256,1024]{1,0:T(8,128)(2,1)S(1)} collective-permute-done((bf16[256,1024]{1,0:T(8,128)(2,1)S(1)}, bf16[256,1024]{1,0:T(8,128)(2,1)S(1)}, u32[]{:S(2)}, u32[]{:S(2)}) %collective-permute-start) | collective-permute-done | bytes 524320 | tf_op jit(solution)/shard_map/while/body/eval_jaxpr/ppermute | solution.py:324
  79.8 1.3 collective-permute-start
  82.2 131.7 %collective-permute-done.inputs = bf16[256,1024]{1,0:T(8,128)(2,1)S(1)} collective-permute-done((bf16[256,1024]{1,0:T(8,128)(2,1)S(1)}, bf16[256,1024]{1,0:T(8,128)(2,1)S(1)}, u32[]{:S(2)}, u32[]{:S(2)}) %collective-permute-start) | collective-permute-done | bytes 524320 | tf_op jit(solution)/shard_map/while/body/eval_jaxpr/ppermute | solution.py:324
  214.8 22.1 %block.7 = bf16[256,1024]{1,0:T(8,128)(2,1)S(1)} custom-call(s32[2]{0:T(128)} %pad_add_fusion.3.info, bf16[256,1024]{1,0:T(8,128)(2,1)} %copy-done.1, f32[40,1024]{1,0:T(8,128)S(1)} %get-tuple-element.336.small, bf16[1,1024,2048]{2,1,0:T(8,128)(2,1)} %get-tuple-element.337.up, ...), custom_call_target="tpu_custom_call", output_to_operand_aliasing={{}: (11, {})} | custom-call | tf_op jit(solution)/shard_map/while/body/eval_jaxpr/block/pallas_call | solution.py:249
  236.9 8.4 %all_to_all.10 = bf16[4,64,1024]{2,1,0:T(8,128)(2,1)S(1)} all-to-all(bf16[4,64,1024]{2,1,0:T(8,128)(2,1)S(1)} %bitcast.14), channel_id=1, replica_groups=mesh['section'=8,'tm'=4] {'tm'}, dimensions={0} | all-to-all | bytes 1048576 | tf_op jit(solution)/shard_map/all_to_all | solution.py:315
  (34 shorter events, 19.4 us)
Async XLA Ops:
  0.0 11.6 %copy-start = (bf16[1,1024,1024]{2,1,0:T(8,128)(2,1)S(1)}, bf16[1,1024,1024]{2,1,0:T(8,128)(2,1)}, u32[]{:S(2)}) copy-start(bf16[1,1024,1024]{2,1,0:T(8,128)(2,1)} %query.1) | copy-start | bytes 6291460
  0.0 10.8 %all-to-all-start = ((bf16[4,64,1024]{2,1,0:T(8,128)(2,1)}), bf16[4,64,1024]{2,1,0:T(8,128)(2,1)S(1)}, u32[]{:S(2)}, u32[]{:S(2)}) async-start(bf16[4,64,1024]{2,1,0:T(8,128)(2,1)} %param.19), calls=%async_computation | async-start | bytes 1048576 | tf_op jit(solution)/shard_map/all_to_all | solution.py:315
  10.8 0.8 copy-start.2
  12.6 5.1 %collective-permute-start = (bf16[256,1024]{1,0:T(8,128)(2,1)S(1)}, bf16[256,1024]{1,0:T(8,128)(2,1)S(1)}, u32[]{:S(2)}, u32[]{:S(2)}) collective-permute-start(bf16[256,1024]{1,0:T(8,128)(2,1)S(1)} %get-tuple-element.319.kept), channel_id=1, source_target_pairs={{0,4},{4,8},{8,12},{12,16},{16,20},{20,24},{24,28},{1,5},{5,9},{9,... | collective-permute-start | bytes 1572872 | tf_op jit(solution)/shard_map/while/body/eval_jaxpr/ppermute | solution.py:324
  17.6 0.8 copy-start.1
  19.3 10.5 %collective-permute-start = (bf16[256,1024]{1,0:T(8,128)(2,1)S(1)}, bf16[256,1024]{1,0:T(8,128)(2,1)S(1)}, u32[]{:S(2)}, u32[]{:S(2)}) collective-permute-start(bf16[256,1024]{1,0:T(8,128)(2,1)S(1)} %get-tuple-element.319.kept), channel_id=1, source_target_pairs={{0,4},{4,8},{8,12},{12,16},{16,20},{20,24},{24,28},{1,5},{5,9},{9,... | collective-permute-start | bytes 1572872 | tf_op jit(solution)/shard_map/while/body/eval_jaxpr/ppermute | solution.py:324
  29.8 0.8 copy-start.1
  31.4 10.5 %collective-permute-start = (bf16[256,1024]{1,0:T(8,128)(2,1)S(1)}, bf16[256,1024]{1,0:T(8,128)(2,1)S(1)}, u32[]{:S(2)}, u32[]{:S(2)}) collective-permute-start(bf16[256,1024]{1,0:T(8,128)(2,1)S(1)} %get-tuple-element.319.kept), channel_id=1, source_target_pairs={{0,4},{4,8},{8,12},{12,16},{16,20},{20,24},{24,28},{1,5},{5,9},{9,... | collective-permute-start | bytes 1572872 | tf_op jit(solution)/shard_map/while/body/eval_jaxpr/ppermute | solution.py:324
  41.9 0.8 copy-start.1
  43.5 10.5 %collective-permute-start = (bf16[256,1024]{1,0:T(8,128)(2,1)S(1)}, bf16[256,1024]{1,0:T(8,128)(2,1)S(1)}, u32[]{:S(2)}, u32[]{:S(2)}) collective-permute-start(bf16[256,1024]{1,0:T(8,128)(2,1)S(1)} %get-tuple-element.319.kept), channel_id=1, source_target_pairs={{0,4},{4,8},{8,12},{12,16},{16,20},{20,24},{24,28},{1,5},{5,9},{9,... | collective-permute-start | bytes 1572872 | tf_op jit(solution)/shard_map/while/body/eval_jaxpr/ppermute | solution.py:324
  54.0 0.8 copy-start.1
  55.6 10.5 %collective-permute-start = (bf16[256,1024]{1,0:T(8,128)(2,1)S(1)}, bf16[256,1024]{1,0:T(8,128)(2,1)S(1)}, u32[]{:S(2)}, u32[]{:S(2)}) collective-permute-start(bf16[256,1024]{1,0:T(8,128)(2,1)S(1)} %get-tuple-element.319.kept), channel_id=1, source_target_pairs={{0,4},{4,8},{8,12},{12,16},{16,20},{20,24},{24,28},{1,5},{5,9},{9,... | collective-permute-start | bytes 1572872 | tf_op jit(solution)/shard_map/while/body/eval_jaxpr/ppermute | solution.py:324
  66.1 0.8 copy-start.1
  67.7 10.5 %collective-permute-start = (bf16[256,1024]{1,0:T(8,128)(2,1)S(1)}, bf16[256,1024]{1,0:T(8,128)(2,1)S(1)}, u32[]{:S(2)}, u32[]{:S(2)}) collective-permute-start(bf16[256,1024]{1,0:T(8,128)(2,1)S(1)} %get-tuple-element.319.kept), channel_id=1, source_target_pairs={{0,4},{4,8},{8,12},{12,16},{16,20},{20,24},{24,28},{1,5},{5,9},{9,... | collective-permute-start | bytes 1572872 | tf_op jit(solution)/shard_map/while/body/eval_jaxpr/ppermute | solution.py:324
  78.2 0.8 copy-start.1
  79.8 134.2 %collective-permute-start = (bf16[256,1024]{1,0:T(8,128)(2,1)S(1)}, bf16[256,1024]{1,0:T(8,128)(2,1)S(1)}, u32[]{:S(2)}, u32[]{:S(2)}) collective-permute-start(bf16[256,1024]{1,0:T(8,128)(2,1)S(1)} %get-tuple-element.319.kept), channel_id=1, source_target_pairs={{0,4},{4,8},{8,12},{12,16},{16,20},{20,24},{24,28},{1,5},{5,9},{9,... | collective-permute-start | bytes 1572872 | tf_op jit(solution)/shard_map/while/body/eval_jaxpr/ppermute | solution.py:324
  214.0 0.8 copy-start.1

commit v2 on v1

v2 whole, which is shorter than its diff:
```python
import math

import jax
import jax.numpy as jnp
from jax import lax
from jax.experimental import pallas as pl
from jax.experimental.pallas import tpu as pltpu
from jax.sharding import PartitionSpec as P

HEADS = 16
EPS = 1e-05
LANES = 128
F32 = jnp.float32
BF16 = jnp.bfloat16


def sigmoid(value):
    return 0.5 * jnp.tanh(0.5 * value) + 0.5


def normalize(value, gain):
    mean = jnp.mean(value, axis=-1, keepdims=True)
    centred = value - mean
    spread = jnp.mean(centred * centred, axis=-1, keepdims=True)
    return centred * lax.rsqrt(spread + EPS) * gain


def dot(left, right):
    return jnp.dot(left, right, preferred_element_type=F32)


def block_kernel(heads, kernel, cols, count):
    def run(info, *refs):
        block_body(info, refs[:count], *refs[count:])

    def block_body(
        info,
        pieces,
        small,
        up,
        down,
        query,
        key,
        value,
        out,
        expand,
        shrink,
        kept,
        result,
        norm_s,
        inner_s,
        start_s,
        q_s,
        k_s,
        v_s,
        glu_s,
        depth_s,
        x_s,
    ):
        length, width = result.shape
        hidden = inner_s.shape[1]
        head = width // heads
        rim = kernel // 2
        pad = (glu_s.shape[0] - length) // 2

        @pl.when(info[0] == 1)
        def active():
            step = 32
            span = min(length, 256)

            def rows_loop(fn):
                def one(i, carry):
                    for j in range(0, span, step):
                        begin = j if span == length else pl.multiple_of(i * span + j, step)
                        fn(pl.ds(begin, step))
                    return carry

                if span == length:
                    one(0, 0)
                else:
                    lax.fori_loop(0, length // span, one, 0)

            inputs = pieces[0]
            if count > 1:
                inputs = x_s
                for i, piece in enumerate(pieces):
                    begin = pl.multiple_of(info[2 + i] * piece.shape[0], piece.shape[0])
                    x_s[pl.ds(begin, piece.shape[0]), :] = piece[...]

            zero = jnp.zeros((pad, width), F32)
            glu_s[0:pad, :] = zero
            glu_s[pad + length : pad + length + pad, :] = zero

            def ffn_norm(at):
                norm_s[at, :] = normalize(inputs[at, :].astype(F32), small[0:1, :]).astype(BF16)

            rows_loop(ffn_norm)
            for j in range(0, hidden, cols):
                part = dot(norm_s[...], up[0, :, j : j + cols])
                inner_s[:, j : j + cols] = (part * sigmoid(part)).astype(BF16)
            for j in range(0, width, cols):
                part = dot(inner_s[...], down[0, :, j : j + cols])
                start_s[:, j : j + cols] = inputs[:, j : j + cols].astype(F32) + 0.5 * part

            def attn_norm(at):
                norm_s[at, :] = normalize(start_s[at, :], small[1:2, :]).astype(BF16)

            rows_loop(attn_norm)
            for weight, target in ((query, q_s), (key, k_s), (value, v_s)):
                for j in range(0, width, cols):
                    target[:, j : j + cols] = dot(norm_s[...], weight[0, :, j : j + cols]).astype(BF16)

            frames = info[1]
            seen = lax.broadcasted_iota(jnp.int32, (1, length), 1) < frames
            lane = lax.broadcasted_iota(jnp.int32, (1, LANES), 1)
            group = LANES // head
            scale = 1.0 / math.sqrt(head)

            def one_group(g, carry):
                at = pl.ds(pl.multiple_of(g * LANES, LANES), LANES)
                queries, keys, values = q_s[:, at], k_s[:, at], v_s[:, at]
                mixed = jnp.zeros((length, 2 * LANES), F32)
                for h in range(group):
                    mine = (lane >= h * head) & (lane < (h + 1) * head)
                    k_head = jnp.where(mine, keys, jnp.zeros_like(keys))
                    scores = lax.dot_general(
                        queries, k_head, (((1,), (1,)), ((), ())), preferred_element_type=F32
                    )
                    scores = jnp.where(seen, scores, -1e30)
                    peak = jnp.max(scores, axis=-1, keepdims=True)
                    weights = jnp.exp2((scores - peak) * (scale * math.log2(math.e))).astype(BF16)
                    v_head = jnp.where(mine, values, jnp.zeros_like(values))
                    ones = jnp.broadcast_to(jnp.where(mine, 1.0, 0.0).astype(BF16), (length, LANES))
                    mixed = mixed + dot(weights, jnp.concatenate([v_head, ones], axis=1))
                norm_s[:, at] = (
                    mixed[:, :LANES] * pl.reciprocal(mixed[:, LANES:], approx=False)
                ).astype(BF16)
                return carry

            groups = width // LANES
            lax.fori_loop(0, groups, one_group, 0, unroll=UNROLL if length <= 256 else 1)

            for j in range(0, width, cols):
                part = dot(norm_s[...], out[0, :, j : j + cols])
                start_s[:, j : j + cols] = start_s[:, j : j + cols] + part

            def conv_norm(at):
                norm_s[at, :] = normalize(start_s[at, :], small[2:3, :]).astype(BF16)

            rows_loop(conv_norm)
            keep = lax.broadcasted_iota(jnp.int32, (length, 1), 0) < frames
            rows = 64
            shift = pad - rim

            def conv(begin, at):
                wide = glu_s[pl.ds(begin, rows + 2 * pad), at]
                total = None
                for r in range(8):
                    taps = [o for o in range(shift, shift + kernel) if o % 8 == r]
                    extent = rows + 8 if r else rows
                    partial = None
                    for o in taps:
                        tap = small[pl.ds(6 + o - shift, 1), at]
                        term = wide[o - r : o - r + extent] * tap
                        partial = term if partial is None else partial + term
                    if r:
                        partial = pltpu.roll(partial, extent - r, 0)[:rows]
                    total = partial if total is None else total + partial
                depth_s[pl.ds(begin, rows), at] = total

            block_cols = cols // 2
            for j in range(0, width, block_cols):
                part = dot(norm_s[...], expand[0, :, j : j + block_cols])
                gate = dot(norm_s[...], expand[0, :, width + j : width + j + block_cols])
                glu = jnp.where(keep, part * sigmoid(gate), 0.0)
                glu_s[pad : pad + length, j : j + block_cols] = glu.astype(BF16).astype(F32)
                for c in range(j, j + block_cols, LANES):
                    for i in range(0, length, rows):
                        conv(i, pl.ds(c, LANES))

            def swish(at):
                shifted = normalize(depth_s[at, :], small[3:4, :]) + small[4:5, :]
                norm_s[at, :] = (shifted * sigmoid(shifted)).astype(BF16)

            rows_loop(swish)
            for j in range(0, width, cols):
                part = dot(norm_s[...], shrink[0, :, j : j + cols])
                start_s[:, j : j + cols] = start_s[:, j : j + cols] + part

            def closing(at):
                result[at, :] = normalize(start_s[at, :], small[5:6, :]).astype(BF16)

            rows_loop(closing)

    return run


UNROLL = 8


def block(info, pieces, small, weights, kept, heads, kernel):
    length, width = kept.shape
    count = len(pieces)
    hidden = weights[0].shape[2]
    cols = 512
    pad = 8 * ((kernel // 2 + 8) // 8)
    vmem = [
        ((length, width), BF16),
        ((length, hidden), BF16),
        ((length, width), F32),
        ((length, width), BF16),
        ((length, width), BF16),
        ((length, width), BF16),
        ((length + 2 * pad, width), F32),
        ((length, width), F32),
        ((length, width), BF16),
    ]
    local = pl.BlockSpec(memory_space=pltpu.VMEM)
    return pl.pallas_call(
        block_kernel(heads, kernel, cols, count),
        out_shape=jax.ShapeDtypeStruct((length, width), BF16),
        in_specs=[pl.BlockSpec(memory_space=pltpu.SMEM)] + [local] * (count + 2 + len(weights)),
        out_specs=local,
        scratch_shapes=[pltpu.VMEM(shape, kind) for shape, kind in vmem],
        input_output_aliases={count + 2 + len(weights): 0},
        compiler_params=pltpu.CompilerParams(vmem_limit_bytes=LIMIT),
        name="block",
    )(info, *pieces, small, *weights, kept)


LIMIT = 30 * 1024 * 1024


def prefetch(info, weights):
    count = len(weights)

    def run(info, *refs):
        sources, targets, sems = refs[:count], refs[count:-1], refs[-1]

        @pl.when(info[0] == 1)
        def active():
            copies = [
                pltpu.make_async_copy(a, b, sems.at[i])
                for i, (a, b) in enumerate(zip(sources, targets))
            ]
            for copy in copies:
                copy.start()
            for copy in copies:
                copy.wait()

    return pl.pallas_call(
        run,
        out_shape=[pltpu.VMEM(w.shape, w.dtype) for w in weights],
        in_specs=[pl.BlockSpec(memory_space=pltpu.SMEM)] + [pl.BlockSpec(memory_space=pl.ANY)] * count,
        out_specs=[pl.BlockSpec(memory_space=pltpu.VMEM)] * len(weights),
        scratch_shapes=[pltpu.SemaphoreType.DMA((len(weights),))],
        compiler_params=pltpu.CompilerParams(vmem_limit_bytes=1024 * 1024),
        name="prefetch",
    )(info, *weights)


def body(
    frames,
    lengths,
    ffn_gain,
    ffn_up,
    ffn_down,
    attn_gain,
    query_weight,
    key_weight,
    value_weight,
    out_weight,
    conv_gain,
    expand_weight,
    depth_weight,
    depth_gain,
    norm_shift,
    shrink_weight,
    final_gain,
):
    sections = lax.axis_size("section")
    section_index = lax.axis_index("section")
    group_index = lax.axis_index("tm")
    micro, rows, width = frames.shape
    peers = lax.axis_size("tm")
    share = peers // micro
    assert share * micro == peers
    utterance = group_index // share
    kernel = depth_weight.shape[1]
    weights = (
        ffn_up,
        ffn_down,
        query_weight,
        key_weight,
        value_weight,
        out_weight,
        expand_weight,
        shrink_weight,
    )
    small = jnp.concatenate(
        [ffn_gain, attn_gain, conv_gain, depth_gain, norm_shift, final_gain, depth_weight[0]]
    )
    small = jnp.pad(small, ((0, -small.shape[0] % 8), (0, 0)))
    length = jnp.sum(jnp.where(jnp.arange(micro, dtype=jnp.int32) == utterance, lengths, 0))
    pairs = [(i, i + 1) for i in range(sections - 1)]
    axes = ("section", "tm")

    def apply(step, pieces, places, kept):
        mine = (step == section_index).astype(jnp.int32)
        info = jnp.stack([mine, length, *places])
        return block(info, pieces, small, prefetch(info, weights), kept, HEADS, kernel)

    pieces = [lax.dynamic_index_in_dim(frames, utterance, 0, keepdims=False)]
    places = [group_index]
    for r in range(1, peers):
        target = (group_index + r) % peers
        part = lax.dynamic_index_in_dim(frames, target // share, 0, keepdims=False)
        pieces.append(lax.ppermute(part, axes, [(j, (j + r) % peers) for j in range(peers)]))
        places.append((group_index - r) % peers)
    kept = apply(0, pieces, places, jnp.zeros((rows * peers, width), frames.dtype))

    def tick(step, kept):
        return apply(step, [lax.ppermute(kept, "section", pairs)], [], kept)

    kept = lax.fori_loop(1, sections, tick, kept)

    def rows_of(index):
        return lax.dynamic_slice_in_dim(kept, index * rows, rows, 0)

    result = jnp.zeros((micro, rows, width), kept.dtype)
    result = lax.dynamic_update_index_in_dim(result, rows_of(group_index), utterance, 0)
    for q in range(1, micro):
        r = q * share
        part = lax.ppermute(
            rows_of((group_index + r) % peers), "tm", [(j, (j + r) % peers) for j in range(peers)]
        )
        source = (group_index - r) % peers // share
        result = lax.dynamic_update_index_in_dim(result, part, source, 0)
    return result[None]


def solution(mesh):
    return jax.shard_map(
        body,
        mesh=mesh,
        in_specs=(
            P(None, "tm", None),
            P(),
            P("section", None),
            P("section", None, None),
            P("section", None, None),
            P("section", None),
            P("section", None, None),
            P("section", None, None),
            P("section", None, None),
            P("section", None, None),
            P("section", None),
            P("section", None, None),
            P("section", None, None),
            P("section", None),
            P("section", None),
            P("section", None, None),
            P("section", None),
        ),
        out_specs=P("section", None, "tm", None),
        check_vma=False,
    )
```

time: 247 us -> 179 us (0.72)
  waiting for transfers between devices: 177 us -> 124 us
  blocking collectives: 8.38 us -> 0 us
  other arithmetic: 10.4 us -> 4.93 us
  local copies, waits for them, and re-layouts: 9.08 us -> 6.15 us
    ppermute x7 -> x13, waiting for transfers between devices: 175 us -> 124 us  [the longest x7 121 us: tick(): return apply(step, [lax.ppermute(kept, 'section', pairs)], [], kept)]
    all_to_all x1 -> x0, blocking collectives: 8.38 us -> none  [exchange(): lax.all_to_all(parts, 'tm', 0, 0, axis_index_groups=across, tiled=True)]
    while x14 -> x0, local copies, waits for them, and re-layouts: 5.55 us -> none
    another operation x8 -> x7, other arithmetic: 9.09 us -> 4.33 us  [apply(): info = jnp.stack([mine, length, *places])]
    ppermute x7 -> x13, starting transfers between devices: 9.04 us -> 13.5 us  [the longest x7 9.04 us: tick(): return apply(step, [lax.ppermute(kept, 'section', pairs)], [], kept)]
    all_to_all x1 -> x0, starting transfers between devices: 3.6 us -> none  [exchange(): lax.all_to_all(parts, 'tm', 0, 0, axis_index_groups=across, tiled=True)]
    all_to_all x1 -> x0, waiting for transfers between devices: 2.78 us -> none  [exchange(): lax.all_to_all(parts, 'tm', 0, 0, axis_index_groups=across, tiled=True)]
    pallas_call x8 -> x16, Pallas kernels: 27.9 us -> 29.4 us  [the longest x8 17.3 us: block(): pl.pallas_call(block_kernel(heads, kernel, cols, count), out_shape=jax.Sh...]
  transfers between devices with their start and end apart: 8 -> 13, of which waited for: 8 -> 9; matrix products, arithmetic and copies ran while one was open for 5% -> 4% of each run, Pallas kernels for 0% -> 7%
where the time goes in v2:
time: 179 us; the launch traced here: 178 us
  waiting for transfers between devices  124 us (69%)
  Pallas kernels  29.4 us (16%)
  starting transfers between devices  13.5 us (8%)
  local copies, waits for them, and re-layouts  6.15 us (3%)
  other arithmetic  4.93 us (3%)
    ppermute x7, waiting for transfers between devices, tick(): return apply(step, [lax.ppermute(kept, 'section', pairs)], [], kept)  121 us
    pallas_call x8, Pallas kernels, block(): pl.pallas_call(block_kernel(heads, kernel, cols, count), out_shape=jax.Sh...  17.3 us
    pallas_call x8, Pallas kernels, prefetch(): pl.pallas_call(run, out_shape=[pltpu.VMEM(w.shape, w.dtype) for w in weig...  12 us
    ppermute x7, starting transfers between devices, tick(): return apply(step, [lax.ppermute(kept, 'section', pairs)], [], kept)  9.04 us
    another operation x7, other arithmetic, apply(): info = jnp.stack([mine, length, *places])  4.33 us
  transfers between devices with their start and end apart: 13, of which 9 were waited for; matrix products, arithmetic and copies ran while one was open for 4% of the time, Pallas kernels for 7%

profile of v2, /device:TPU:25, one launch (start us, length us, event | category | flops | bytes accessed | tf_op | source)
XLA Modules:
  0.0 178.3 jit_solution(2690835155190112790)
XLA Ops:
  0.0 1.9 %dynamic-slice_bitcast_fusion = (bf16[64,1024]{1,0:T(8,128)(2,1)S(1)}, bf16[64,1024]{1,0:T(8,128)(2,1)}, bf16[64,1024]{1,0:T(8,128)(2,1)S(1)}, bf16[64,1024]{1,0:T(8,128)(2,1)S(1)}) fusion(bf16[4,64,1024]{2,1,0:T(8,128)(2,1)} %param.19, s32[]{:T(128)S(6)} %select_n.97, s32[]{:T(128)S(6)} %select_n.93, s32[]{:T(128)S(6)} %select_n.91, s32[]{:T(128)S(6)} %select_n.95), kind=kLoop, calls=%fused_computation.6 | loop fusion | bytes 1048592 | tf_op jit(solution)/shard_map/jit(dynamic_index_in_dim)/squeeze | solution.py:317
  4.0 0.9 copy.22
  5.0 1.0 concatenate.3
  8.0 0.7 block.6
  8.8 162.4 %while.13 = (s32[]{:T(128)}, bf16[256,1024]{1,0:T(8,128)(2,1)S(1)}, s32[]{:T(128)}, s32[]{:T(128)}, bf16[1,1024,2048]{2,1,0:T(8,128)(2,1)}, /*index=5*/bf16[1,20...) while((s32[]{:T(128)}, bf16[256,1024]{1,0:T(8,128)(2,1)S(1)}, ...), condition=%wide.region_2.3_spmd, body=%wide.region_1.2_spmd.sunk | while | flops 6 | bytes 2097355 | solution.py:325
  8.8 1.3 collective-permute-start
  11.3 1.4 collective-permute-done.refs_0_
  13.3 1.3 collective-permute-start
  15.9 7.9 %collective-permute-done.refs_0_ = bf16[256,1024]{1,0:T(8,128)(2,1)S(1)} collective-permute-done((bf16[256,1024]{1,0:T(8,128)(2,1)S(1)}, bf16[256,1024]{1,0:T(8,128)(2,1)S(1)}, u32[]{:S(2)}, u32[]{:S(2)}) %collective-permute-start) | collective-permute-done | bytes 524320 | tf_op jit(solution)/shard_map/while/body/eval_jaxpr/ppermute | solution.py:323
  24.4 1.3 collective-permute-start
  26.9 7.9 %collective-permute-done.refs_0_ = bf16[256,1024]{1,0:T(8,128)(2,1)S(1)} collective-permute-done((bf16[256,1024]{1,0:T(8,128)(2,1)S(1)}, bf16[256,1024]{1,0:T(8,128)(2,1)S(1)}, u32[]{:S(2)}, u32[]{:S(2)}) %collective-permute-start) | collective-permute-done | bytes 524320 | tf_op jit(solution)/shard_map/while/body/eval_jaxpr/ppermute | solution.py:323
  35.5 1.3 collective-permute-start
  38.0 7.9 %collective-permute-done.refs_0_ = bf16[256,1024]{1,0:T(8,128)(2,1)S(1)} collective-permute-done((bf16[256,1024]{1,0:T(8,128)(2,1)S(1)}, bf16[256,1024]{1,0:T(8,128)(2,1)S(1)}, u32[]{:S(2)}, u32[]{:S(2)}) %collective-permute-start) | collective-permute-done | bytes 524320 | tf_op jit(solution)/shard_map/while/body/eval_jaxpr/ppermute | solution.py:323
  46.5 1.3 collective-permute-start
  49.1 7.9 %collective-permute-done.refs_0_ = bf16[256,1024]{1,0:T(8,128)(2,1)S(1)} collective-permute-done((bf16[256,1024]{1,0:T(8,128)(2,1)S(1)}, bf16[256,1024]{1,0:T(8,128)(2,1)S(1)}, u32[]{:S(2)}, u32[]{:S(2)}) %collective-permute-start) | collective-permute-done | bytes 524320 | tf_op jit(solution)/shard_map/while/body/eval_jaxpr/ppermute | solution.py:323
  57.6 1.3 collective-permute-start
  60.1 7.9 %collective-permute-done.refs_0_ = bf16[256,1024]{1,0:T(8,128)(2,1)S(1)} collective-permute-done((bf16[256,1024]{1,0:T(8,128)(2,1)S(1)}, bf16[256,1024]{1,0:T(8,128)(2,1)S(1)}, u32[]{:S(2)}, u32[]{:S(2)}) %collective-permute-start) | collective-permute-done | bytes 524320 | tf_op jit(solution)/shard_map/while/body/eval_jaxpr/ppermute | solution.py:323
  68.7 1.3 collective-permute-start
  70.6 7.7 %prefetch.7 = (bf16[1,1024,2048]{2,1,0:T(8,128)(2,1)S(1)}, bf16[1,2048,1024]{2,1,0:T(8,128)(2,1)S(1)}, bf16[1,1024,1024]{2,1,0:T(8,128)(2,1)S(1)}, bf16[1,1024,1...) custom-call(s32[2]{0:T(128)S(1)} %pad_add_fusion.2.info, ...), custom_call_target="tpu_custom_call" | custom-call | tf_op jit(solution)/shard_map/while/body/eval_jaxpr/prefetch/pallas_call | solution.py:251
  78.3 79.6 %collective-permute-done.refs_0_ = bf16[256,1024]{1,0:T(8,128)(2,1)S(1)} collective-permute-done((bf16[256,1024]{1,0:T(8,128)(2,1)S(1)}, bf16[256,1024]{1,0:T(8,128)(2,1)S(1)}, u32[]{:S(2)}, u32[]{:S(2)}) %collective-permute-start) | collective-permute-done | bytes 524320 | tf_op jit(solution)/shard_map/while/body/eval_jaxpr/ppermute | solution.py:323
  157.9 13.3 %block.7 = bf16[256,1024]{1,0:T(8,128)(2,1)S(1)} custom-call(s32[2]{0:T(128)S(1)} %pad_add_fusion.2.info, bf16[256,1024]{1,0:T(8,128)(2,1)S(1)} %collective-permute-done.refs_0_, f32[40,1024]{1,0:T(8,128)S(1)} %get-tuple-element.391.refs_1_, bf16[1,1024,2048]{2,1,0:T(8,128)(2,1)S(1)} %get-tuple-element.343.refs_2_, ...), custom_call_target="tpu_custom_call", output_to_operand_aliasing={{}: (11, {})} | custom-call | tf_op jit(solution)/shard_map/while/body/eval_jaxpr/block/pallas_call | solution.py:219
  171.8 1.8 %collective-permute-start.6 = (bf16[64,1024]{1,0:T(8,128)(2,1)S(1)}, bf16[64,1024]{1,0:T(8,128)(2,1)S(1)}, u32[]{:S(2)}, u32[]{:S(2)}) collective-permute-start(bf16[64,1024]{1,0:T(8,128)(2,1)S(1)} %get-tuple-element.249), channel_id=1, source_target_pairs={{0,3},{1,0},{2,1},{3,2},{4,7},{5,4},{6,5},{7,6},{8,11},{9,8},{10,9... | collective-permute-start | bytes 393224 | tf_op jit(solution)/shard_map/ppermute | solution.py:334
  173.7 2.4 %collective-permute-done.4 = bf16[64,1024]{1,0:T(8,128)(2,1)S(1)} collective-permute-done((bf16[64,1024]{1,0:T(8,128)(2,1)S(1)}, bf16[64,1024]{1,0:T(8,128)(2,1)S(1)}, u32[]{:S(2)}, u32[]{:S(2)}) %collective-permute-start.4) | collective-permute-done | bytes 131104 | tf_op jit(solution)/shard_map/ppermute | solution.py:334
  176.9 0.8 copy-done.1
  (45 shorter events, 17.3 us)
Async XLA Ops:
  0.0 6.1 %copy-start.2 = (s32[4]{0:T(128)S(1)}, s32[4]{0:T(128)}, u32[]{:S(2)}) copy-start(s32[4]{0:T(128)} %param.20) | copy-start | bytes 52
  0.0 7.3 %copy-start = (bf16[1,1024,1024]{2,1,0:T(8,128)(2,1)S(1)}, bf16[1,1024,1024]{2,1,0:T(8,128)(2,1)}, u32[]{:S(2)}) copy-start(bf16[1,1024,1024]{2,1,0:T(8,128)(2,1)} %refs_2_.1) | copy-start | bytes 6291460
  1.9 6.0 %collective-permute-start.1 = (bf16[64,1024]{1,0:T(8,128)(2,1)}, bf16[64,1024]{1,0:T(8,128)(2,1)S(1)}, u32[]{:S(2)}, u32[]{:S(2)}) collective-permute-start(bf16[64,1024]{1,0:T(8,128)(2,1)} %get-tuple-element.253), channel_id=1, source_target_pairs={{0,1},{1,2},{2,3},{3,0}} | collective-permute-start | bytes 393224 | tf_op jit(solution)/shard_map/ppermute | solution.py:318
  2.6 5.3 %collective-permute-start.2 = (bf16[64,1024]{1,0:T(8,128)(2,1)S(1)}, bf16[64,1024]{1,0:T(8,128)(2,1)S(1)}, u32[]{:S(2)}, u32[]{:S(2)}) collective-permute-start(bf16[64,1024]{1,0:T(8,128)(2,1)S(1)} %get-tuple-element.255), channel_id=1, source_target_pairs={{0,2},{1,3},{2,0},{3,1}} | collective-permute-start | bytes 393224 | tf_op jit(solution)/shard_map/ppermute | solution.py:318
  3.3 4.7 %collective-permute-start.3 = (bf16[64,1024]{1,0:T(8,128)(2,1)S(1)}, bf16[64,1024]{1,0:T(8,128)(2,1)S(1)}, u32[]{:S(2)}, u32[]{:S(2)}) collective-permute-start(bf16[64,1024]{1,0:T(8,128)(2,1)S(1)} %get-tuple-element.252), channel_id=1, source_target_pairs={{0,3},{1,0},{2,1},{3,2}} | collective-permute-start | bytes 393224 | tf_op jit(solution)/shard_map/ppermute | solution.py:318
  8.8 4.0 %collective-permute-start = (bf16[256,1024]{1,0:T(8,128)(2,1)S(1)}, bf16[256,1024]{1,0:T(8,128)(2,1)S(1)}, u32[]{:S(2)}, u32[]{:S(2)}) collective-permute-start(bf16[256,1024]{1,0:T(8,128)(2,1)S(1)} %get-tuple-element.366.refs_10_), channel_id=1, source_target_pairs={{0,4},{4,8},{8,12},{12,16},{16,20},{20,24},{24,28},{1,5},{5,9},{9,... | collective-permute-start | bytes 1572872 | tf_op jit(solution)/shard_map/while/body/eval_jaxpr/ppermute | solution.py:323
  13.3 10.5 %collective-permute-start = (bf16[256,1024]{1,0:T(8,128)(2,1)S(1)}, bf16[256,1024]{1,0:T(8,128)(2,1)S(1)}, u32[]{:S(2)}, u32[]{:S(2)}) collective-permute-start(bf16[256,1024]{1,0:T(8,128)(2,1)S(1)} %get-tuple-element.366.refs_10_), channel_id=1, source_target_pairs={{0,4},{4,8},{8,12},{12,16},{16,20},{20,24},{24,28},{1,5},{5,9},{9,... | collective-permute-start | bytes 1572872 | tf_op jit(solution)/shard_map/while/body/eval_jaxpr/ppermute | solution.py:323
  24.4 10.5 %collective-permute-start = (bf16[256,1024]{1,0:T(8,128)(2,1)S(1)}, bf16[256,1024]{1,0:T(8,128)(2,1)S(1)}, u32[]{:S(2)}, u32[]{:S(2)}) collective-permute-start(bf16[256,1024]{1,0:T(8,128)(2,1)S(1)} %get-tuple-element.366.refs_10_), channel_id=1, source_target_pairs={{0,4},{4,8},{8,12},{12,16},{16,20},{20,24},{24,28},{1,5},{5,9},{9,... | collective-permute-start | bytes 1572872 | tf_op jit(solution)/shard_map/while/body/eval_jaxpr/ppermute | solution.py:323
  35.5 10.5 %collective-permute-start = (bf16[256,1024]{1,0:T(8,128)(2,1)S(1)}, bf16[256,1024]{1,0:T(8,128)(2,1)S(1)}, u32[]{:S(2)}, u32[]{:S(2)}) collective-permute-start(bf16[256,1024]{1,0:T(8,128)(2,1)S(1)} %get-tuple-element.366.refs_10_), channel_id=1, source_target_pairs={{0,4},{4,8},{8,12},{12,16},{16,20},{20,24},{24,28},{1,5},{5,9},{9,... | collective-permute-start | bytes 1572872 | tf_op jit(solution)/shard_map/while/body/eval_jaxpr/ppermute | solution.py:323
  46.5 10.5 %collective-permute-start = (bf16[256,1024]{1,0:T(8,128)(2,1)S(1)}, bf16[256,1024]{1,0:T(8,128)(2,1)S(1)}, u32[]{:S(2)}, u32[]{:S(2)}) collective-permute-start(bf16[256,1024]{1,0:T(8,128)(2,1)S(1)} %get-tuple-element.366.refs_10_), channel_id=1, source_target_pairs={{0,4},{4,8},{8,12},{12,16},{16,20},{20,24},{24,28},{1,5},{5,9},{9,... | collective-permute-start | bytes 1572872 | tf_op jit(solution)/shard_map/while/body/eval_jaxpr/ppermute | solution.py:323
  57.6 10.5 %collective-permute-start = (bf16[256,1024]{1,0:T(8,128)(2,1)S(1)}, bf16[256,1024]{1,0:T(8,128)(2,1)S(1)}, u32[]{:S(2)}, u32[]{:S(2)}) collective-permute-start(bf16[256,1024]{1,0:T(8,128)(2,1)S(1)} %get-tuple-element.366.refs_10_), channel_id=1, source_target_pairs={{0,4},{4,8},{8,12},{12,16},{16,20},{20,24},{24,28},{1,5},{5,9},{9,... | collective-permute-start | bytes 1572872 | tf_op jit(solution)/shard_map/while/body/eval_jaxpr/ppermute | solution.py:323
  68.7 89.2 %collective-permute-start = (bf16[256,1024]{1,0:T(8,128)(2,1)S(1)}, bf16[256,1024]{1,0:T(8,128)(2,1)S(1)}, u32[]{:S(2)}, u32[]{:S(2)}) collective-permute-start(bf16[256,1024]{1,0:T(8,128)(2,1)S(1)} %get-tuple-element.366.refs_10_), channel_id=1, source_target_pairs={{0,4},{4,8},{8,12},{12,16},{16,20},{20,24},{24,28},{1,5},{5,9},{9,... | collective-permute-start | bytes 1572872 | tf_op jit(solution)/shard_map/while/body/eval_jaxpr/ppermute | solution.py:323
  171.2 4.9 %collective-permute-start.4 = (bf16[64,1024]{1,0:T(8,128)(2,1)S(1)}, bf16[64,1024]{1,0:T(8,128)(2,1)S(1)}, u32[]{:S(2)}, u32[]{:S(2)}) collective-permute-start(bf16[64,1024]{1,0:T(8,128)(2,1)S(1)} %get-tuple-element.251), channel_id=1, source_target_pairs={{0,1},{1,2},{2,3},{3,0},{4,5},{5,6},{6,7},{7,4},{8,9},{9,10},{10,1... | collective-permute-start | bytes 393224 | tf_op jit(solution)/shard_map/ppermute | solution.py:334
  171.6 5.2 %collective-permute-start.5 = (bf16[64,1024]{1,0:T(8,128)(2,1)S(1)}, bf16[64,1024]{1,0:T(8,128)(2,1)S(1)}, u32[]{:S(2)}, u32[]{:S(2)}) collective-permute-start(bf16[64,1024]{1,0:T(8,128)(2,1)S(1)} %get-tuple-element.250), channel_id=1, source_target_pairs={{0,2},{1,3},{2,0},{3,1},{4,6},{5,7},{6,4},{7,5},{8,10},{9,11},{10,... | collective-permute-start | bytes 393224 | tf_op jit(solution)/shard_map/ppermute | solution.py:334
  171.8 5.0 %collective-permute-start.6 = (bf16[64,1024]{1,0:T(8,128)(2,1)S(1)}, bf16[64,1024]{1,0:T(8,128)(2,1)S(1)}, u32[]{:S(2)}, u32[]{:S(2)}) collective-permute-start(bf16[64,1024]{1,0:T(8,128)(2,1)S(1)} %get-tuple-element.249), channel_id=1, source_target_pairs={{0,3},{1,0},{2,1},{3,2},{4,7},{5,4},{6,5},{7,6},{8,11},{9,8},{10,9... | collective-permute-start | bytes 393224 | tf_op jit(solution)/shard_map/ppermute | solution.py:334
  176.8 0.8 copy-start.1

commit v3 on v2

v3 whole, which is shorter than its diff:
```python
import math

import jax
import jax.numpy as jnp
from jax import lax
from jax.experimental import pallas as pl
from jax.experimental.pallas import tpu as pltpu
from jax.sharding import PartitionSpec as P

HEADS = 16
EPS = 1e-05
LANES = 128
F32 = jnp.float32
BF16 = jnp.bfloat16


def sigmoid(value):
    return 0.5 * jnp.tanh(0.5 * value) + 0.5


def normalize(value, gain):
    mean = jnp.mean(value, axis=-1, keepdims=True)
    centred = value - mean
    spread = jnp.mean(centred * centred, axis=-1, keepdims=True)
    return centred * lax.rsqrt(spread + EPS) * gain


def dot(left, right):
    return jnp.dot(left, right, preferred_element_type=F32)


UP, DOWN, QUERY, KEY, VALUE, OUT, EXPAND, SHRINK = range(8)
COLS = 512


def pieces_of(index, shape):
    if index in (UP, DOWN):
        return [(0, slice(None), pl.ds(j, COLS)) for j in range(0, shape[2], COLS)]
    return [(0,)]


def block_kernel(heads, count, held, utterance_of, first, places):
    def run(*refs):
        refs = list(refs)

        def take(n):
            taken = refs[:n]
            del refs[:n]
            return taken

        (step, lengths) = take(2)
        pieces = take(count)
        params = take(held)
        take(1)
        (result,) = take(1)
        (norm_s, inner_s, start_s, q_s, k_s, v_s, glu_s, depth_s) = take(8)
        cols = COLS
        length, width = result.shape
        hidden = inner_s.shape[1]
        head = width // heads
        pad = (glu_s.shape[1] - length) // 2
        utterance = utterance_of()
        mine = lax.axis_index("section") == (0 if first else step[0])

        @pl.when(mine)
        def active():
            step_rows = 32
            span = min(length, 256)

            def rows_loop(fn):
                def one(i, carry):
                    for j in range(0, span, step_rows):
                        begin = j if span == length else pl.multiple_of(i * span + j, step_rows)
                        fn(pl.ds(begin, step_rows))
                    return carry

                if span == length:
                    one(0, 0)
                else:
                    lax.fori_loop(0, length // span, one, 0)

            inputs = pieces[0]
            local = params
            copies = {}
            if first:
                (inputs,) = take(1)
                local = take(held)
                (sems,) = take(1)
                order = list(range(8, held)) + list(range(8))
                for index in order:
                    shape = params[index].shape
                    parts = pieces_of(index, shape) if index < 8 else [(0,)]
                    for part in parts:
                        copy = pltpu.make_async_copy(
                            params[index].at[part],
                            local[index].at[part],
                            sems.at[sum(map(len, copies.values()))],
                        )
                        copy.start()
                        copies.setdefault(index, []).append(copy)
                for i, piece in enumerate(pieces):
                    begin = pl.multiple_of(places(i) * piece.shape[0], piece.shape[0])
                    inputs[pl.ds(begin, piece.shape[0]), :] = piece[...]
                for index in range(8, held):
                    copies[index][0].wait()

            def wait(index, column=0):
                if first and column // COLS < len(copies[index]):
                    copies[index][column // COLS].wait()

            weights = local[:8]
            (up, down, query, key, value, out, expand, shrink) = weights
            gains = local[8:14]
            taps = local[14]
            kernel = taps.shape[1]
            rim = kernel // 2

            zero = jnp.zeros((width // LANES, pad, LANES), F32)
            glu_s[:, 0:pad, :] = zero
            glu_s[:, pad + length : pad + length + pad, :] = zero

            def ffn_norm(at):
                norm_s[at, :] = normalize(inputs[at, :].astype(F32), gains[0][...]).astype(BF16)

            rows_loop(ffn_norm)
            for j in range(0, hidden, cols):
                wait(UP, j)
                part = dot(norm_s[...], up[0, :, j : j + cols])
                inner_s[:, j : j + cols] = (part * sigmoid(part)).astype(BF16)
            for j in range(0, width, cols):
                wait(DOWN, j)
                part = dot(inner_s[...], down[0, :, j : j + cols])
                start_s[:, j : j + cols] = inputs[:, j : j + cols].astype(F32) + 0.5 * part

            def attn_norm(at):
                norm_s[at, :] = normalize(start_s[at, :], gains[1][...]).astype(BF16)

            rows_loop(attn_norm)
            for which, target in ((QUERY, q_s), (KEY, k_s), (VALUE, v_s)):
                weight = weights[which]
                wait(which)
                for j in range(0, width, cols):
                    target[:, j : j + cols] = dot(norm_s[...], weight[0, :, j : j + cols]).astype(BF16)

            frames = lengths[utterance]
            seen = lax.broadcasted_iota(jnp.int32, (1, length), 1) < frames
            lane = lax.broadcasted_iota(jnp.int32, (1, LANES), 1)
            group = LANES // head
            scale = 1.0 / math.sqrt(head)

            def one_group(g, carry):
                at = pl.ds(pl.multiple_of(g * LANES, LANES), LANES)
                queries, keys, values = q_s[:, at], k_s[:, at], v_s[:, at]
                mixed = jnp.zeros((length, 2 * LANES), F32)
                for h in range(group):
                    mine = (lane >= h * head) & (lane < (h + 1) * head)
                    k_head = jnp.where(mine, keys, jnp.zeros_like(keys))
                    scores = lax.dot_general(
                        queries, k_head, (((1,), (1,)), ((), ())), preferred_element_type=F32
                    )
                    scores = jnp.where(seen, scores, -1e30)
                    peak = jnp.max(scores, axis=-1, keepdims=True)
                    weights = jnp.exp2((scores - peak) * (scale * math.log2(math.e))).astype(BF16)
                    v_head = jnp.where(mine, values, jnp.zeros_like(values))
                    ones = jnp.broadcast_to(jnp.where(mine, 1.0, 0.0).astype(BF16), (length, LANES))
                    mixed = mixed + dot(weights, jnp.concatenate([v_head, ones], axis=1))
                norm_s[:, at] = (
                    mixed[:, :LANES] * pl.reciprocal(mixed[:, LANES:], approx=False)
                ).astype(BF16)
                return carry

            groups = width // LANES
            lax.fori_loop(0, groups, one_group, 0, unroll=UNROLL if length <= 256 else 1)

            wait(OUT)
            for j in range(0, width, cols):
                part = dot(norm_s[...], out[0, :, j : j + cols])
                start_s[:, j : j + cols] = start_s[:, j : j + cols] + part

            def conv_norm(at):
                norm_s[at, :] = normalize(start_s[at, :], gains[2][...]).astype(BF16)

            rows_loop(conv_norm)
            keep = lax.broadcasted_iota(jnp.int32, (length, 1), 0) < frames
            rows = 256
            shift = pad - rim

            def conv(begin, slab):
                at = pl.ds(pl.multiple_of(slab * LANES, LANES), LANES)
                total = None
                for r in range(8):
                    offsets = range(r, kernel, 8)
                    wide = glu_s[slab, pl.ds(begin + shift + r, rows + 8 * (len(offsets) - 1)), :]
                    for i, o in enumerate(offsets):
                        term = wide[8 * i : 8 * i + rows] * taps[0, pl.ds(o, 1), at]
                        total = term if total is None else total + term
                depth_s[pl.ds(begin, rows), at] = total

            block_cols = cols // 2
            wait(EXPAND)
            for j in range(0, width, block_cols):
                part = dot(norm_s[...], expand[0, :, j : j + block_cols])
                gate = dot(norm_s[...], expand[0, :, width + j : width + j + block_cols])
                glu = jnp.where(keep, part * sigmoid(gate), 0.0)
                glu = glu.astype(BF16).astype(F32)
                for c in range(0, block_cols, LANES):
                    slab = (j + c) // LANES
                    glu_s[slab, pad : pad + length, :] = glu[:, c : c + LANES]

            chunks = length // rows

            def conv_step(i, carry):
                conv(pl.multiple_of(i % chunks * rows, rows), i // chunks)
                return carry

            lax.fori_loop(0, chunks * (width // LANES), conv_step, 0)

            def swish(at):
                shifted = normalize(depth_s[at, :], gains[3][...]) + gains[4][...]
                norm_s[at, :] = (shifted * sigmoid(shifted)).astype(BF16)

            rows_loop(swish)
            wait(SHRINK)
            for j in range(0, width, cols):
                part = dot(norm_s[...], shrink[0, :, j : j + cols])
                start_s[:, j : j + cols] = start_s[:, j : j + cols] + part

            def closing(at):
                result[at, :] = normalize(start_s[at, :], gains[5][...]).astype(BF16)

            rows_loop(closing)

    return run


UNROLL = 8


def block(step, lengths, places, pieces, params, kept, heads, utterance_of):
    length, width = kept.shape
    hidden = params[UP].shape[2]
    kernel = params[14].shape[1]
    count, held, first = len(pieces), len(params), step is None
    pad = 8 * ((kernel // 2 + 8) // 8)
    vmem = [
        ((length, width), BF16),
        ((length, hidden), BF16),
        ((length, width), F32),
        ((length, width), BF16),
        ((length, width), BF16),
        ((length, width), BF16),
        ((width // LANES, length + 2 * pad, LANES), F32),
        ((length, width), F32),
    ]
    scalars = [jnp.zeros((1,), jnp.int32) if first else step, lengths]
    sems = []
    if first:
        vmem += [((length, width), BF16)] + [(p.shape, p.dtype) for p in params]
        total = held - 8 + sum(len(pieces_of(i, params[i].shape)) for i in range(8))
        sems = [pltpu.SemaphoreType.DMA((total,))]
    local = pl.BlockSpec(memory_space=pltpu.VMEM)
    return pl.pallas_call(
        block_kernel(heads, count, held, utterance_of, first, places),
        out_shape=jax.ShapeDtypeStruct((length, width), BF16),
        in_specs=[pl.BlockSpec(memory_space=pltpu.SMEM)] * len(scalars)
        + [local] * count
        + [pl.BlockSpec(memory_space=pl.ANY) if first else local] * held
        + [local],
        out_specs=local,
        scratch_shapes=[pltpu.VMEM(shape, kind) for shape, kind in vmem] + sems,
        input_output_aliases={len(scalars) + count + held: 0},
        compiler_params=pltpu.CompilerParams(
            vmem_limit_bytes=(40 if first else 30) * 1024 * 1024
        ),
        name="block",
    )(*scalars, *pieces, *params, kept)


def prefetch(step, params):
    count = len(params)

    def run(step, *refs):
        sources, targets, sems = refs[:count], refs[count:-1], refs[-1]

        @pl.when(lax.axis_index("section") == step[0])
        def active():
            copies = [
                pltpu.make_async_copy(a, b, sems.at[i])
                for i, (a, b) in enumerate(zip(sources, targets))
            ]
            for copy in copies:
                copy.start()
            for copy in copies:
                copy.wait()

    return pl.pallas_call(
        run,
        out_shape=[pltpu.VMEM(p.shape, p.dtype) for p in params],
        in_specs=[pl.BlockSpec(memory_space=pltpu.SMEM)] + [pl.BlockSpec(memory_space=pl.ANY)] * count,
        out_specs=[pl.BlockSpec(memory_space=pltpu.VMEM)] * count,
        scratch_shapes=[pltpu.SemaphoreType.DMA((count,))],
        compiler_params=pltpu.CompilerParams(vmem_limit_bytes=1024 * 1024),
        name="prefetch",
    )(step, *params)


def body(
    frames,
    lengths,
    ffn_gain,
    ffn_up,
    ffn_down,
    attn_gain,
    query_weight,
    key_weight,
    value_weight,
    out_weight,
    conv_gain,
    expand_weight,
    depth_weight,
    depth_gain,
    norm_shift,
    shrink_weight,
    final_gain,
):
    sections = lax.axis_size("section")
    group_index = lax.axis_index("tm")
    micro, rows, width = frames.shape
    peers = lax.axis_size("tm")
    share = peers // micro
    assert share * micro == peers
    utterance = group_index // share
    params = (
        ffn_up,
        ffn_down,
        query_weight,
        key_weight,
        value_weight,
        out_weight,
        expand_weight,
        shrink_weight,
        ffn_gain,
        attn_gain,
        conv_gain,
        depth_gain,
        norm_shift,
        final_gain,
        depth_weight,
    )
    pairs = [(i, i + 1) for i in range(sections - 1)]
    axes = ("section", "tm")

    def utterance_of():
        return lax.axis_index("tm") // share

    def source_of(r):
        return lax.rem(lax.axis_index("tm") + (peers - r), peers)

    pieces = [lax.dynamic_index_in_dim(frames, utterance, 0, keepdims=False)]
    for r in range(1, peers):
        target = (group_index + r) % peers
        part = lax.dynamic_index_in_dim(frames, target // share, 0, keepdims=False)
        pieces.append(lax.ppermute(part, axes, [(j, (j + r) % peers) for j in range(peers)]))
    kept = jnp.zeros((rows * peers, width), frames.dtype)
    kept = block(None, lengths, source_of, pieces, params, kept, HEADS, utterance_of)

    def tick(step, kept):
        step = jnp.reshape(step, (1,))
        pieces = [lax.ppermute(kept, "section", pairs)]
        held = prefetch(step, params)
        return block(step, lengths, None, pieces, held, kept, HEADS, utterance_of)

    kept = lax.fori_loop(1, sections, tick, kept)

    def rows_of(index):
        return lax.dynamic_slice_in_dim(kept, index * rows, rows, 0)

    result = jnp.zeros((micro, rows, width), kept.dtype)
    result = lax.dynamic_update_index_in_dim(result, rows_of(group_index), utterance, 0)
    for q in range(1, micro):
        r = q * share
        part = lax.ppermute(
            rows_of((group_index + r) % peers), "tm", [(j, (j + r) % peers) for j in range(peers)]
        )
        source = (group_index - r) % peers // share
        result = lax.dynamic_update_index_in_dim(result, part, source, 0)
    return result[None]


def solution(mesh):
    return jax.shard_map(
        body,
        mesh=mesh,
        in_specs=(
            P(None, "tm", None),
            P(),
            P("section", None),
            P("section", None, None),
            P("section", None, None),
            P("section", None),
            P("section", None, None),
            P("section", None, None),
            P("section", None, None),
            P("section", None, None),
            P("section", None),
            P("section", None, None),
            P("section", None, None),
            P("section", None),
            P("section", None),
            P("section", None, None),
            P("section", None),
        ),
        out_specs=P("section", None, "tm", None),
        check_vma=False,
    )
```

time: 179 us -> 168 us (0.939)
  other arithmetic: 4.93 us -> 0 us
  Pallas kernels: 29.4 us -> 25.4 us
  local copies, waits for them, and re-layouts: 6.15 us -> 4.03 us
    another operation x7 -> x0, other arithmetic: 4.33 us -> none  [apply(): info = jnp.stack([mine, length, *places])]
    pallas_call x16 -> x15, Pallas kernels: 29.4 us -> 25.4 us  [the longest x8 16.8 us: block(): pl.pallas_call(block_kernel(heads, count, held, utterance_of, first, plac...]
  transfers between devices with their start and end apart: 13 -> 13, of which waited for: 9 -> 9; matrix products, arithmetic and copies ran while one was open for 4% -> 1% of each run, Pallas kernels for 7% -> 5%
where the time goes in v3:
time: 168 us
  waiting for transfers between devices  124 us (74%)
  Pallas kernels  25.4 us (15%)
  starting transfers between devices  13.7 us (8%)
  local copies, waits for them, and re-layouts  4.03 us (2%)
    ppermute x7, waiting for transfers between devices, tick(): pieces = [lax.ppermute(kept, 'section', pairs)]  121 us
    pallas_call x8, Pallas kernels, block(): pl.pallas_call(block_kernel(heads, count, held, utterance_of, first, plac...  16.8 us
    ppermute x7, starting transfers between devices, tick(): pieces = [lax.ppermute(kept, 'section', pairs)]  9.04 us
    pallas_call x7, Pallas kernels, prefetch(): pl.pallas_call(run, out_shape=[pltpu.VMEM(p.shape, p.dtype) for p in para...  8.58 us
    ppermute x3, waiting for transfers between devices, body(): lax.ppermute(rows_of((group_index + r) % peers), 'tm', [(j, (j + r) % pee...  3.43 us
  transfers between devices with their start and end apart: 13, of which 9 were waited for; matrix products, arithmetic and copies ran while one was open for 1% of the time, Pallas kernels for 5%

profile of v3, /device:TPU:25, one launch (start us, length us, event | category | flops | bytes accessed | tf_op | source)
XLA Modules:
  0.0 167.7 jit_solution(2156751157191130307)
XLA Ops:
  0.0 1.1 dynamic-slice_bitcast_fusion
  3.2 0.9 copy.20.refs_20_
  4.3 1.2 block.6
  5.9 154.1 %while.13 = (s32[]{:T(128)}, bf16[256,1024]{1,0:T(8,128)(2,1)S(1)}, bf16[1,1024,2048]{2,1,0:T(8,128)(2,1)}, bf16[1,2048,1024]{2,1,0:T(8,128)(2,1)}, bf16[1,1024,...) while((s32[]{:T(128)}, bf16[256,1024]{1,0:T(8,128)(2,1)S(1)}, ...), condition=%wide.region_1.2_spmd, body=%wide.region_0.1_spmd.sunk | while | flops 2 | bytes 2097365 | solution.py:373
  5.9 1.3 collective-permute-start
  7.4 2.5 %collective-permute-done.refs_2_ = bf16[256,1024]{1,0:T(8,128)(2,1)S(1)} collective-permute-done((bf16[256,1024]{1,0:T(8,128)(2,1)S(1)}, bf16[256,1024]{1,0:T(8,128)(2,1)S(1)}, u32[]{:S(2)}, u32[]{:S(2)}) %collective-permute-start) | collective-permute-done | bytes 524320 | tf_op jit(solution)/shard_map/while/body/eval_jaxpr/ppermute | solution.py:369
  10.4 1.3 collective-permute-start
  11.9 9.0 %collective-permute-done.refs_2_ = bf16[256,1024]{1,0:T(8,128)(2,1)S(1)} collective-permute-done((bf16[256,1024]{1,0:T(8,128)(2,1)S(1)}, bf16[256,1024]{1,0:T(8,128)(2,1)S(1)}, u32[]{:S(2)}, u32[]{:S(2)}) %collective-permute-start) | collective-permute-done | bytes 524320 | tf_op jit(solution)/shard_map/while/body/eval_jaxpr/ppermute | solution.py:369
  21.5 1.3 collective-permute-start
  23.0 9.0 %collective-permute-done.refs_2_ = bf16[256,1024]{1,0:T(8,128)(2,1)S(1)} collective-permute-done((bf16[256,1024]{1,0:T(8,128)(2,1)S(1)}, bf16[256,1024]{1,0:T(8,128)(2,1)S(1)}, u32[]{:S(2)}, u32[]{:S(2)}) %collective-permute-start) | collective-permute-done | bytes 524320 | tf_op jit(solution)/shard_map/while/body/eval_jaxpr/ppermute | solution.py:369
  32.6 1.3 collective-permute-start
  34.1 9.0 %collective-permute-done.refs_2_ = bf16[256,1024]{1,0:T(8,128)(2,1)S(1)} collective-permute-done((bf16[256,1024]{1,0:T(8,128)(2,1)S(1)}, bf16[256,1024]{1,0:T(8,128)(2,1)S(1)}, u32[]{:S(2)}, u32[]{:S(2)}) %collective-permute-start) | collective-permute-done | bytes 524320 | tf_op jit(solution)/shard_map/while/body/eval_jaxpr/ppermute | solution.py:369
  43.6 1.3 collective-permute-start
  45.2 9.0 %collective-permute-done.refs_2_ = bf16[256,1024]{1,0:T(8,128)(2,1)S(1)} collective-permute-done((bf16[256,1024]{1,0:T(8,128)(2,1)S(1)}, bf16[256,1024]{1,0:T(8,128)(2,1)S(1)}, u32[]{:S(2)}, u32[]{:S(2)}) %collective-permute-start) | collective-permute-done | bytes 524320 | tf_op jit(solution)/shard_map/while/body/eval_jaxpr/ppermute | solution.py:369
  54.7 1.3 collective-permute-start
  56.2 9.0 %collective-permute-done.refs_2_ = bf16[256,1024]{1,0:T(8,128)(2,1)S(1)} collective-permute-done((bf16[256,1024]{1,0:T(8,128)(2,1)S(1)}, bf16[256,1024]{1,0:T(8,128)(2,1)S(1)}, u32[]{:S(2)}, u32[]{:S(2)}) %collective-permute-start) | collective-permute-done | bytes 524320 | tf_op jit(solution)/shard_map/while/body/eval_jaxpr/ppermute | solution.py:369
  65.8 1.3 collective-permute-start
  67.1 7.3 %prefetch.5 = (bf16[1,1024,2048]{2,1,0:T(8,128)(2,1)S(1)}, bf16[1,2048,1024]{2,1,0:T(8,128)(2,1)S(1)}, bf16[1,1024,1024]{2,1,0:T(8,128)(2,1)S(1)}, bf16[1,1024,1...) custom-call(s32[1]{0:T(128)} %bitcast.18.step.refs_0_, ...), custom_call_target="tpu_custom_call" | custom-call | tf_op jit(solution)/shard_map/while/body/eval_jaxpr/prefetch/pallas_call | solution.py:296
  74.4 73.3 %collective-permute-done.refs_2_ = bf16[256,1024]{1,0:T(8,128)(2,1)S(1)} collective-permute-done((bf16[256,1024]{1,0:T(8,128)(2,1)S(1)}, bf16[256,1024]{1,0:T(8,128)(2,1)S(1)}, u32[]{:S(2)}, u32[]{:S(2)}) %collective-permute-start) | collective-permute-done | bytes 524320 | tf_op jit(solution)/shard_map/while/body/eval_jaxpr/ppermute | solution.py:369
  147.7 12.3 %block.7 = bf16[256,1024]{1,0:T(8,128)(2,1)S(1)} custom-call(s32[1]{0:T(128)} %bitcast.18.step.refs_0_, s32[4]{0:T(128)S(1)} %get-tuple-element.530.refs_1_, bf16[256,1024]{1,0:T(8,128)(2,1)S(1)} %collective-permute-done.refs_2_, bf16[1,1024,2048]{2,1,0:T(8,128)(2,1)S(1)} %get-tuple-element.460.refs_3_, ...), custom_call_target="tpu_custom_call", output_to_operand_aliasing={{}: (18, {})} | custom-call | tf_op jit(solution)/shard_map/while/body/eval_jaxpr/block/pallas_call | solution.py:262
  160.7 1.7 %collective-permute-start.5 = (bf16[64,1024]{1,0:T(8,128)(2,1)S(1)}, bf16[64,1024]{1,0:T(8,128)(2,1)S(1)}, u32[]{:S(2)}, u32[]{:S(2)}) collective-permute-start(bf16[64,1024]{1,0:T(8,128)(2,1)S(1)} %get-tuple-element.330), channel_id=1, source_target_pairs={{0,2},{1,3},{2,0},{3,1},{4,6},{5,7},{6,4},{7,5},{8,10},{9,11},{10,... | collective-permute-start | bytes 393224 | tf_op jit(solution)/shard_map/ppermute | solution.py:382
  162.8 2.1 %collective-permute-done.4 = bf16[64,1024]{1,0:T(8,128)(2,1)S(1)} collective-permute-done((bf16[64,1024]{1,0:T(8,128)(2,1)S(1)}, bf16[64,1024]{1,0:T(8,128)(2,1)S(1)}, u32[]{:S(2)}, u32[]{:S(2)}) %collective-permute-start.4) | collective-permute-done | bytes 131104 | tf_op jit(solution)/shard_map/ppermute | solution.py:382
  164.9 1.3 collective-permute-done.5
  166.2 0.8 copy-done.1
  (45 shorter events, 8.8 us)
Async XLA Ops:
  1.1 3.0 %collective-permute-start.1 = (bf16[64,1024]{1,0:T(8,128)(2,1)S(1)}, bf16[64,1024]{1,0:T(8,128)(2,1)S(1)}, u32[]{:S(2)}, u32[]{:S(2)}) collective-permute-start(bf16[64,1024]{1,0:T(8,128)(2,1)S(1)} %get-tuple-element.333), channel_id=1, source_target_pairs={{0,1},{1,2},{2,3},{3,0}} | collective-permute-start | bytes 393224 | tf_op jit(solution)/shard_map/ppermute | solution.py:363
  1.8 2.3 %collective-permute-start.2 = (bf16[64,1024]{1,0:T(8,128)(2,1)S(1)}, bf16[64,1024]{1,0:T(8,128)(2,1)S(1)}, u32[]{:S(2)}, u32[]{:S(2)}) collective-permute-start(bf16[64,1024]{1,0:T(8,128)(2,1)S(1)} %get-tuple-element.335), channel_id=1, source_target_pairs={{0,2},{1,3},{2,0},{3,1}} | collective-permute-start | bytes 393224 | tf_op jit(solution)/shard_map/ppermute | solution.py:363
  2.5 1.7 collective-permute-start.3
  4.2 1.6 copy-start
  4.2 1.6 copy-start.2
  4.2 1.6 copy-start.3
  4.3 1.6 copy-start.4
  4.3 1.6 copy-start.5
  4.3 1.6 copy-start.6
  4.3 1.5 copy-start.7
  4.3 1.5 copy-start.8
  5.9 4.0 %collective-permute-start = (bf16[256,1024]{1,0:T(8,128)(2,1)S(1)}, bf16[256,1024]{1,0:T(8,128)(2,1)S(1)}, u32[]{:S(2)}, u32[]{:S(2)}) collective-permute-start(bf16[256,1024]{1,0:T(8,128)(2,1)S(1)} %get-tuple-element.495.refs_18_), channel_id=1, source_target_pairs={{0,4},{4,8},{8,12},{12,16},{16,20},{20,24},{24,28},{1,5},{5,9},{9,... | collective-permute-start | bytes 1572872 | tf_op jit(solution)/shard_map/while/body/eval_jaxpr/ppermute | solution.py:369
  10.4 10.5 %collective-permute-start = (bf16[256,1024]{1,0:T(8,128)(2,1)S(1)}, bf16[256,1024]{1,0:T(8,128)(2,1)S(1)}, u32[]{:S(2)}, u32[]{:S(2)}) collective-permute-start(bf16[256,1024]{1,0:T(8,128)(2,1)S(1)} %get-tuple-element.495.refs_18_), channel_id=1, source_target_pairs={{0,4},{4,8},{8,12},{12,16},{16,20},{20,24},{24,28},{1,5},{5,9},{9,... | collective-permute-start | bytes 1572872 | tf_op jit(solution)/shard_map/while/body/eval_jaxpr/ppermute | solution.py:369
  21.5 10.5 %collective-permute-start = (bf16[256,1024]{1,0:T(8,128)(2,1)S(1)}, bf16[256,1024]{1,0:T(8,128)(2,1)S(1)}, u32[]{:S(2)}, u32[]{:S(2)}) collective-permute-start(bf16[256,1024]{1,0:T(8,128)(2,1)S(1)} %get-tuple-element.495.refs_18_), channel_id=1, source_target_pairs={{0,4},{4,8},{8,12},{12,16},{16,20},{20,24},{24,28},{1,5},{5,9},{9,... | collective-permute-start | bytes 1572872 | tf_op jit(solution)/shard_map/while/body/eval_jaxpr/ppermute | solution.py:369
  32.6 10.5 %collective-permute-start = (bf16[256,1024]{1,0:T(8,128)(2,1)S(1)}, bf16[256,1024]{1,0:T(8,128)(2,1)S(1)}, u32[]{:S(2)}, u32[]{:S(2)}) collective-permute-start(bf16[256,1024]{1,0:T(8,128)(2,1)S(1)} %get-tuple-element.495.refs_18_), channel_id=1, source_target_pairs={{0,4},{4,8},{8,12},{12,16},{16,20},{20,24},{24,28},{1,5},{5,9},{9,... | collective-permute-start | bytes 1572872 | tf_op jit(solution)/shard_map/while/body/eval_jaxpr/ppermute | solution.py:369
  43.6 10.5 %collective-permute-start = (bf16[256,1024]{1,0:T(8,128)(2,1)S(1)}, bf16[256,1024]{1,0:T(8,128)(2,1)S(1)}, u32[]{:S(2)}, u32[]{:S(2)}) collective-permute-start(bf16[256,1024]{1,0:T(8,128)(2,1)S(1)} %get-tuple-element.495.refs_18_), channel_id=1, source_target_pairs={{0,4},{4,8},{8,12},{12,16},{16,20},{20,24},{24,28},{1,5},{5,9},{9,... | collective-permute-start | bytes 1572872 | tf_op jit(solution)/shard_map/while/body/eval_jaxpr/ppermute | solution.py:369
  54.7 10.5 %collective-permute-start = (bf16[256,1024]{1,0:T(8,128)(2,1)S(1)}, bf16[256,1024]{1,0:T(8,128)(2,1)S(1)}, u32[]{:S(2)}, u32[]{:S(2)}) collective-permute-start(bf16[256,1024]{1,0:T(8,128)(2,1)S(1)} %get-tuple-element.495.refs_18_), channel_id=1, source_target_pairs={{0,4},{4,8},{8,12},{12,16},{16,20},{20,24},{24,28},{1,5},{5,9},{9,... | collective-permute-start | bytes 1572872 | tf_op jit(solution)/shard_map/while/body/eval_jaxpr/ppermute | solution.py:369
  65.8 81.9 %collective-permute-start = (bf16[256,1024]{1,0:T(8,128)(2,1)S(1)}, bf16[256,1024]{1,0:T(8,128)(2,1)S(1)}, u32[]{:S(2)}, u32[]{:S(2)}) collective-permute-start(bf16[256,1024]{1,0:T(8,128)(2,1)S(1)} %get-tuple-element.495.refs_18_), channel_id=1, source_target_pairs={{0,4},{4,8},{8,12},{12,16},{16,20},{20,24},{24,28},{1,5},{5,9},{9,... | collective-permute-start | bytes 1572872 | tf_op jit(solution)/shard_map/while/body/eval_jaxpr/ppermute | solution.py:369
  160.0 4.9 %collective-permute-start.4 = (bf16[64,1024]{1,0:T(8,128)(2,1)S(1)}, bf16[64,1024]{1,0:T(8,128)(2,1)S(1)}, u32[]{:S(2)}, u32[]{:S(2)}) collective-permute-start(bf16[64,1024]{1,0:T(8,128)(2,1)S(1)} %get-tuple-element.331), channel_id=1, source_target_pairs={{0,1},{1,2},{2,3},{3,0},{4,5},{5,6},{6,7},{7,4},{8,9},{9,10},{10,1... | collective-permute-start | bytes 393224 | tf_op jit(solution)/shard_map/ppermute | solution.py:382
  160.7 5.5 %collective-permute-start.5 = (bf16[64,1024]{1,0:T(8,128)(2,1)S(1)}, bf16[64,1024]{1,0:T(8,128)(2,1)S(1)}, u32[]{:S(2)}, u32[]{:S(2)}) collective-permute-start(bf16[64,1024]{1,0:T(8,128)(2,1)S(1)} %get-tuple-element.330), channel_id=1, source_target_pairs={{0,2},{1,3},{2,0},{3,1},{4,6},{5,7},{6,4},{7,5},{8,10},{9,11},{10,... | collective-permute-start | bytes 393224 | tf_op jit(solution)/shard_map/ppermute | solution.py:382
  162.4 3.8 %collective-permute-start.6 = (bf16[64,1024]{1,0:T(8,128)(2,1)S(1)}, bf16[64,1024]{1,0:T(8,128)(2,1)S(1)}, u32[]{:S(2)}, u32[]{:S(2)}) collective-permute-start(bf16[64,1024]{1,0:T(8,128)(2,1)S(1)} %get-tuple-element.329), channel_id=1, source_target_pairs={{0,3},{1,0},{2,1},{3,2},{4,7},{5,4},{6,5},{7,6},{8,11},{9,8},{10,9... | collective-permute-start | bytes 393224 | tf_op jit(solution)/shard_map/ppermute | solution.py:382
  166.2 0.8 copy-start.1

commit v4 on v3

--- a/solution.py
+++ b/solution.py
@@ -83,7 +83,8 @@
             local = params
             copies = {}
             if first:
-                (inputs,) = take(1)
+                (assembled,) = take(1)
+                inputs = assembled if count > 1 else inputs
                 local = take(held)
                 (sems,) = take(1)
                 order = list(range(8, held)) + list(range(8))
@@ -98,9 +99,9 @@
                         )
                         copy.start()
                         copies.setdefault(index, []).append(copy)
-                for i, piece in enumerate(pieces):
+                for i, piece in enumerate(pieces if count > 1 else []):
                     begin = pl.multiple_of(places(i) * piece.shape[0], piece.shape[0])
-                    inputs[pl.ds(begin, piece.shape[0]), :] = piece[...]
+                    assembled[pl.ds(begin, piece.shape[0]), :] = piece[...]
                 for index in range(8, held):
                     copies[index][0].wait()
 
@@ -140,13 +141,15 @@
                 weight = weights[which]
                 wait(which)
                 for j in range(0, width, cols):
-                    target[:, j : j + cols] = dot(norm_s[...], weight[0, :, j : j + cols]).astype(BF16)
+                    part = dot(norm_s[...], weight[0, :, j : j + cols])
+                    if which == QUERY:
+                        part = part * (math.log2(math.e) / math.sqrt(head))
+                    target[:, j : j + cols] = part.astype(BF16)
 
             frames = lengths[utterance]
             seen = lax.broadcasted_iota(jnp.int32, (1, length), 1) < frames
             lane = lax.broadcasted_iota(jnp.int32, (1, LANES), 1)
             group = LANES // head
-            scale = 1.0 / math.sqrt(head)
 
             def one_group(g, carry):
                 at = pl.ds(pl.multiple_of(g * LANES, LANES), LANES)
@@ -160,7 +163,7 @@
                     )
                     scores = jnp.where(seen, scores, -1e30)
                     peak = jnp.max(scores, axis=-1, keepdims=True)
-                    weights = jnp.exp2((scores - peak) * (scale * math.log2(math.e))).astype(BF16)
+                    weights = jnp.exp2(scores - peak).astype(BF16)
                     v_head = jnp.where(mine, values, jnp.zeros_like(values))
                     ones = jnp.broadcast_to(jnp.where(mine, 1.0, 0.0).astype(BF16), (length, LANES))
                     mixed = mixed + dot(weights, jnp.concatenate([v_head, ones], axis=1))
@@ -356,11 +359,15 @@
     def source_of(r):
         return lax.rem(lax.axis_index("tm") + (peers - r), peers)
 
-    pieces = [lax.dynamic_index_in_dim(frames, utterance, 0, keepdims=False)]
-    for r in range(1, peers):
-        target = (group_index + r) % peers
-        part = lax.dynamic_index_in_dim(frames, target // share, 0, keepdims=False)
-        pieces.append(lax.ppermute(part, axes, [(j, (j + r) % peers) for j in range(peers)]))
+    if share == 1:
+        own = lax.all_to_all(frames, "tm", 0, 0, tiled=True)
+        pieces = [own.reshape(rows * peers, width)]
+    else:
+        pieces = [lax.dynamic_index_in_dim(frames, utterance, 0, keepdims=False)]
+        for r in range(1, peers):
+            target = (group_index + r) % peers
+            part = lax.dynamic_index_in_dim(frames, target // share, 0, keepdims=False)
+            pieces.append(lax.ppermute(part, axes, [(j, (j + r) % peers) for j in range(peers)]))
     kept = jnp.zeros((rows * peers, width), frames.dtype)
     kept = block(None, lengths, source_of, pieces, params, kept, HEADS, utterance_of)
 

time: 168 us -> 165 us (0.982)
  waiting for transfers between devices: 124 us -> 119 us
  starting transfers between devices: 13.7 us -> 16.1 us
    ppermute x7, waiting for transfers between devices: 121 us -> 111 us  [tick(): pieces = [lax.ppermute(kept, 'section', pairs)]]
    all_to_all x0 -> x1, waiting for transfers between devices: none -> 6.19 us  [body(): own = lax.all_to_all(frames, 'tm', 0, 0, tiled=True)]
    all_to_all x0 -> x1, starting transfers between devices: none -> 3.47 us  [body(): own = lax.all_to_all(frames, 'tm', 0, 0, tiled=True)]
    ppermute x3 -> x0, starting transfers between devices: 2.01 us -> none  [body(): lax.ppermute(part, axes, [(j, (j + r) % peers) for j in range(peers)])]
  transfers between devices with their start and end apart: 13 -> 11, of which waited for: 9 -> 10; matrix products, arithmetic and copies ran while one was open for 1% -> 1% of each run, Pallas kernels for 5% -> 5%
where the time goes in v4:
time: 165 us; the launch traced here: 164 us
  waiting for transfers between devices  119 us (72%)
  Pallas kernels  25.3 us (15%)
  starting transfers between devices  16.1 us (10%)
  local copies, waits for them, and re-layouts  2.89 us (2%)
    ppermute x7, waiting for transfers between devices, tick(): pieces = [lax.ppermute(kept, 'section', pairs)]  111 us
    pallas_call x8, Pallas kernels, block(): pl.pallas_call(block_kernel(heads, count, held, utterance_of, first, plac...  16.8 us
    ppermute x7, starting transfers between devices, tick(): pieces = [lax.ppermute(kept, 'section', pairs)]  9.04 us
    pallas_call x7, Pallas kernels, prefetch(): pl.pallas_call(run, out_shape=[pltpu.VMEM(p.shape, p.dtype) for p in para...  8.58 us
    all_to_all x1, waiting for transfers between devices, body(): own = lax.all_to_all(frames, 'tm', 0, 0, tiled=True)  6.19 us
    ppermute x3, starting transfers between devices, body(): lax.ppermute(rows_of((group_index + r) % peers), 'tm', [(j, (j + r) % pee...  3.62 us
    all_to_all x1, starting transfers between devices, body(): own = lax.all_to_all(frames, 'tm', 0, 0, tiled=True)  3.47 us
  transfers between devices with their start and end apart: 11, of which 10 were waited for; matrix products, arithmetic and copies ran while one was open for 1% of the time, Pallas kernels for 5%

profile of v4, /device:TPU:25, one launch (start us, length us, event | category | flops | bytes accessed | tf_op | source)
XLA Modules:
  0.0 164.3 jit_solution(4765286741381573080)
XLA Ops:
  0.0 3.5 %all-to-all-start = ((bf16[4,64,1024]{2,1,0:T(8,128)(2,1)}), bf16[4,64,1024]{2,1,0:T(8,128)(2,1)S(1)}, u32[]{:S(2)}, u32[]{:S(2)}) async-start(bf16[4,64,1024]{2,1,0:T(8,128)(2,1)} %param.19), calls=%async_computation | async-start | bytes 1048576 | tf_op jit(solution)/shard_map/all_to_all | solution.py:363
  4.5 6.2 %all-to-all-done = bf16[4,64,1024]{2,1,0:T(8,128)(2,1)S(1)} async-done(((bf16[4,64,1024]{2,1,0:T(8,128)(2,1)}), bf16[4,64,1024]{2,1,0:T(8,128)(2,1)S(1)}, u32[]{:S(2)}, u32[]{:S(2)}) %all-to-all-start) | async-done | bytes 524320 | tf_op jit(solution)/shard_map/all_to_all | solution.py:363
  10.8 1.2 block.6
  12.4 144.3 %while.13 = (s32[]{:T(128)}, bf16[256,1024]{1,0:T(8,128)(2,1)S(1)}, bf16[1,1024,2048]{2,1,0:T(8,128)(2,1)}, bf16[1,2048,1024]{2,1,0:T(8,128)(2,1)}, bf16[1,1024,...) while((s32[]{:T(128)}, bf16[256,1024]{1,0:T(8,128)(2,1)S(1)}, ...), condition=%wide.region_1.2_spmd, body=%wide.region_0.1_spmd.sunk | while | flops 2 | bytes 2097365 | solution.py:380
  12.4 1.3 collective-permute-start
  13.9 3.5 %collective-permute-done.refs_2_ = bf16[256,1024]{1,0:T(8,128)(2,1)S(1)} collective-permute-done((bf16[256,1024]{1,0:T(8,128)(2,1)S(1)}, bf16[256,1024]{1,0:T(8,128)(2,1)S(1)}, u32[]{:S(2)}, u32[]{:S(2)}) %collective-permute-start) | collective-permute-done | bytes 524320 | tf_op jit(solution)/shard_map/while/body/eval_jaxpr/ppermute | solution.py:376
  18.0 1.3 collective-permute-start
  19.5 9.0 %collective-permute-done.refs_2_ = bf16[256,1024]{1,0:T(8,128)(2,1)S(1)} collective-permute-done((bf16[256,1024]{1,0:T(8,128)(2,1)S(1)}, bf16[256,1024]{1,0:T(8,128)(2,1)S(1)}, u32[]{:S(2)}, u32[]{:S(2)}) %collective-permute-start) | collective-permute-done | bytes 524320 | tf_op jit(solution)/shard_map/while/body/eval_jaxpr/ppermute | solution.py:376
  29.1 1.3 collective-permute-start
  30.6 9.0 %collective-permute-done.refs_2_ = bf16[256,1024]{1,0:T(8,128)(2,1)S(1)} collective-permute-done((bf16[256,1024]{1,0:T(8,128)(2,1)S(1)}, bf16[256,1024]{1,0:T(8,128)(2,1)S(1)}, u32[]{:S(2)}, u32[]{:S(2)}) %collective-permute-start) | collective-permute-done | bytes 524320 | tf_op jit(solution)/shard_map/while/body/eval_jaxpr/ppermute | solution.py:376
  40.1 1.3 collective-permute-start
  41.7 9.0 %collective-permute-done.refs_2_ = bf16[256,1024]{1,0:T(8,128)(2,1)S(1)} collective-permute-done((bf16[256,1024]{1,0:T(8,128)(2,1)S(1)}, bf16[256,1024]{1,0:T(8,128)(2,1)S(1)}, u32[]{:S(2)}, u32[]{:S(2)}) %collective-permute-start) | collective-permute-done | bytes 524320 | tf_op jit(solution)/shard_map/while/body/eval_jaxpr/ppermute | solution.py:376
  51.2 1.3 collective-permute-start
  52.7 9.0 %collective-permute-done.refs_2_ = bf16[256,1024]{1,0:T(8,128)(2,1)S(1)} collective-permute-done((bf16[256,1024]{1,0:T(8,128)(2,1)S(1)}, bf16[256,1024]{1,0:T(8,128)(2,1)S(1)}, u32[]{:S(2)}, u32[]{:S(2)}) %collective-permute-start) | collective-permute-done | bytes 524320 | tf_op jit(solution)/shard_map/while/body/eval_jaxpr/ppermute | solution.py:376
  62.3 1.3 collective-permute-start
  63.8 9.0 %collective-permute-done.refs_2_ = bf16[256,1024]{1,0:T(8,128)(2,1)S(1)} collective-permute-done((bf16[256,1024]{1,0:T(8,128)(2,1)S(1)}, bf16[256,1024]{1,0:T(8,128)(2,1)S(1)}, u32[]{:S(2)}, u32[]{:S(2)}) %collective-permute-start) | collective-permute-done | bytes 524320 | tf_op jit(solution)/shard_map/while/body/eval_jaxpr/ppermute | solution.py:376
  73.4 1.3 collective-permute-start
  74.7 7.3 %prefetch.5 = (bf16[1,1024,2048]{2,1,0:T(8,128)(2,1)S(1)}, bf16[1,2048,1024]{2,1,0:T(8,128)(2,1)S(1)}, bf16[1,1024,1024]{2,1,0:T(8,128)(2,1)S(1)}, bf16[1,1024,1...) custom-call(s32[1]{0:T(128)} %bitcast.11.step.refs_0_, ...), custom_call_target="tpu_custom_call" | custom-call | tf_op jit(solution)/shard_map/while/body/eval_jaxpr/prefetch/pallas_call | solution.py:299
  82.0 62.4 %collective-permute-done.refs_2_ = bf16[256,1024]{1,0:T(8,128)(2,1)S(1)} collective-permute-done((bf16[256,1024]{1,0:T(8,128)(2,1)S(1)}, bf16[256,1024]{1,0:T(8,128)(2,1)S(1)}, u32[]{:S(2)}, u32[]{:S(2)}) %collective-permute-start) | collective-permute-done | bytes 524320 | tf_op jit(solution)/shard_map/while/body/eval_jaxpr/ppermute | solution.py:376
  144.3 12.3 %block.7 = bf16[256,1024]{1,0:T(8,128)(2,1)S(1)} custom-call(s32[1]{0:T(128)} %bitcast.11.step.refs_0_, s32[4]{0:T(128)S(1)} %get-tuple-element.526.refs_1_, bf16[256,1024]{1,0:T(8,128)(2,1)S(1)} %collective-permute-done.refs_2_, bf16[1,1024,2048]{2,1,0:T(8,128)(2,1)S(1)} %get-tuple-element.456.refs_3_, ...), custom_call_target="tpu_custom_call", output_to_operand_aliasing={{}: (18, {})} | custom-call | tf_op jit(solution)/shard_map/while/body/eval_jaxpr/block/pallas_call | solution.py:265
  156.7 1.2 collective-permute-start.1
  158.2 2.1 %collective-permute-start.3 = (bf16[64,1024]{1,0:T(8,128)(2,1)S(1)}, bf16[64,1024]{1,0:T(8,128)(2,1)S(1)}, u32[]{:S(2)}, u32[]{:S(2)}) collective-permute-start(bf16[64,1024]{1,0:T(8,128)(2,1)S(1)} %get-tuple-element.329), channel_id=1, source_target_pairs={{0,3},{1,0},{2,1},{3,2},{4,7},{5,4},{6,5},{7,6},{8,11},{9,8},{10,9... | collective-permute-start | bytes 393224 | tf_op jit(solution)/shard_map/ppermute | solution.py:389
  160.4 1.2 collective-permute-done.1
  161.6 1.3 collective-permute-done.2
  (40 shorter events, 7.8 us)
Async XLA Ops:
  0.0 10.7 %all-to-all-start = ((bf16[4,64,1024]{2,1,0:T(8,128)(2,1)}), bf16[4,64,1024]{2,1,0:T(8,128)(2,1)S(1)}, u32[]{:S(2)}, u32[]{:S(2)}) async-start(bf16[4,64,1024]{2,1,0:T(8,128)(2,1)} %param.19), calls=%async_computation | async-start | bytes 1048576 | tf_op jit(solution)/shard_map/all_to_all | solution.py:363
  10.7 1.6 copy-start
  10.7 1.6 copy-start.2
  10.7 1.6 copy-start.3
  10.7 1.6 copy-start.4
  10.8 1.6 copy-start.5
  10.8 1.6 copy-start.6
  10.8 1.5 copy-start.7
  10.8 1.5 copy-start.8
  12.4 5.1 %collective-permute-start = (bf16[256,1024]{1,0:T(8,128)(2,1)S(1)}, bf16[256,1024]{1,0:T(8,128)(2,1)S(1)}, u32[]{:S(2)}, u32[]{:S(2)}) collective-permute-start(bf16[256,1024]{1,0:T(8,128)(2,1)S(1)} %get-tuple-element.491.refs_18_), channel_id=1, source_target_pairs={{0,4},{4,8},{8,12},{12,16},{16,20},{20,24},{24,28},{1,5},{5,9},{9,... | collective-permute-start | bytes 1572872 | tf_op jit(solution)/shard_map/while/body/eval_jaxpr/ppermute | solution.py:376
  18.0 10.5 %collective-permute-start = (bf16[256,1024]{1,0:T(8,128)(2,1)S(1)}, bf16[256,1024]{1,0:T(8,128)(2,1)S(1)}, u32[]{:S(2)}, u32[]{:S(2)}) collective-permute-start(bf16[256,1024]{1,0:T(8,128)(2,1)S(1)} %get-tuple-element.491.refs_18_), channel_id=1, source_target_pairs={{0,4},{4,8},{8,12},{12,16},{16,20},{20,24},{24,28},{1,5},{5,9},{9,... | collective-permute-start | bytes 1572872 | tf_op jit(solution)/shard_map/while/body/eval_jaxpr/ppermute | solution.py:376
  29.1 10.5 %collective-permute-start = (bf16[256,1024]{1,0:T(8,128)(2,1)S(1)}, bf16[256,1024]{1,0:T(8,128)(2,1)S(1)}, u32[]{:S(2)}, u32[]{:S(2)}) collective-permute-start(bf16[256,1024]{1,0:T(8,128)(2,1)S(1)} %get-tuple-element.491.refs_18_), channel_id=1, source_target_pairs={{0,4},{4,8},{8,12},{12,16},{16,20},{20,24},{24,28},{1,5},{5,9},{9,... | collective-permute-start | bytes 1572872 | tf_op jit(solution)/shard_map/while/body/eval_jaxpr/ppermute | solution.py:376
  40.1 10.5 %collective-permute-start = (bf16[256,1024]{1,0:T(8,128)(2,1)S(1)}, bf16[256,1024]{1,0:T(8,128)(2,1)S(1)}, u32[]{:S(2)}, u32[]{:S(2)}) collective-permute-start(bf16[256,1024]{1,0:T(8,128)(2,1)S(1)} %get-tuple-element.491.refs_18_), channel_id=1, source_target_pairs={{0,4},{4,8},{8,12},{12,16},{16,20},{20,24},{24,28},{1,5},{5,9},{9,... | collective-permute-start | bytes 1572872 | tf_op jit(solution)/shard_map/while/body/eval_jaxpr/ppermute | solution.py:376
  51.2 10.5 %collective-permute-start = (bf16[256,1024]{1,0:T(8,128)(2,1)S(1)}, bf16[256,1024]{1,0:T(8,128)(2,1)S(1)}, u32[]{:S(2)}, u32[]{:S(2)}) collective-permute-start(bf16[256,1024]{1,0:T(8,128)(2,1)S(1)} %get-tuple-element.491.refs_18_), channel_id=1, source_target_pairs={{0,4},{4,8},{8,12},{12,16},{16,20},{20,24},{24,28},{1,5},{5,9},{9,... | collective-permute-start | bytes 1572872 | tf_op jit(solution)/shard_map/while/body/eval_jaxpr/ppermute | solution.py:376
  62.3 10.5 %collective-permute-start = (bf16[256,1024]{1,0:T(8,128)(2,1)S(1)}, bf16[256,1024]{1,0:T(8,128)(2,1)S(1)}, u32[]{:S(2)}, u32[]{:S(2)}) collective-permute-start(bf16[256,1024]{1,0:T(8,128)(2,1)S(1)} %get-tuple-element.491.refs_18_), channel_id=1, source_target_pairs={{0,4},{4,8},{8,12},{12,16},{16,20},{20,24},{24,28},{1,5},{5,9},{9,... | collective-permute-start | bytes 1572872 | tf_op jit(solution)/shard_map/while/body/eval_jaxpr/ppermute | solution.py:376
  73.4 71.0 %collective-permute-start = (bf16[256,1024]{1,0:T(8,128)(2,1)S(1)}, bf16[256,1024]{1,0:T(8,128)(2,1)S(1)}, u32[]{:S(2)}, u32[]{:S(2)}) collective-permute-start(bf16[256,1024]{1,0:T(8,128)(2,1)S(1)} %get-tuple-element.491.refs_18_), channel_id=1, source_target_pairs={{0,4},{4,8},{8,12},{12,16},{16,20},{20,24},{24,28},{1,5},{5,9},{9,... | collective-permute-start | bytes 1572872 | tf_op jit(solution)/shard_map/while/body/eval_jaxpr/ppermute | solution.py:376
  156.7 4.9 %collective-permute-start.1 = (bf16[64,1024]{1,0:T(8,128)(2,1)S(1)}, bf16[64,1024]{1,0:T(8,128)(2,1)S(1)}, u32[]{:S(2)}, u32[]{:S(2)}) collective-permute-start(bf16[64,1024]{1,0:T(8,128)(2,1)S(1)} %get-tuple-element.331), channel_id=1, source_target_pairs={{0,1},{1,2},{2,3},{3,0},{4,5},{5,6},{6,7},{7,4},{8,9},{9,10},{10,1... | collective-permute-start | bytes 393224 | tf_op jit(solution)/shard_map/ppermute | solution.py:389
  157.9 5.0 %collective-permute-start.2 = (bf16[64,1024]{1,0:T(8,128)(2,1)S(1)}, bf16[64,1024]{1,0:T(8,128)(2,1)S(1)}, u32[]{:S(2)}, u32[]{:S(2)}) collective-permute-start(bf16[64,1024]{1,0:T(8,128)(2,1)S(1)} %get-tuple-element.330), channel_id=1, source_target_pairs={{0,2},{1,3},{2,0},{3,1},{4,6},{5,7},{6,4},{7,5},{8,10},{9,11},{10,... | collective-permute-start | bytes 393224 | tf_op jit(solution)/shard_map/ppermute | solution.py:389
  158.2 4.8 %collective-permute-start.3 = (bf16[64,1024]{1,0:T(8,128)(2,1)S(1)}, bf16[64,1024]{1,0:T(8,128)(2,1)S(1)}, u32[]{:S(2)}, u32[]{:S(2)}) collective-permute-start(bf16[64,1024]{1,0:T(8,128)(2,1)S(1)} %get-tuple-element.329), channel_id=1, source_target_pairs={{0,3},{1,0},{2,1},{3,2},{4,7},{5,4},{6,5},{7,6},{8,11},{9,8},{10,9... | collective-permute-start | bytes 393224 | tf_op jit(solution)/shard_map/ppermute | solution.py:389
  162.9 0.8 copy-start.1

commit v5 on v4

--- a/solution.py
+++ b/solution.py
@@ -31,6 +31,7 @@
 
 UP, DOWN, QUERY, KEY, VALUE, OUT, EXPAND, SHRINK = range(8)
 COLS = 512
+WINDOW = 5 * 1024 * 1024
 
 
 def pieces_of(index, shape):
@@ -87,27 +88,45 @@
                 inputs = assembled if count > 1 else inputs
                 local = take(held)
                 (sems,) = take(1)
-                order = list(range(8, held)) + list(range(8))
-                for index in order:
-                    shape = params[index].shape
-                    parts = pieces_of(index, shape) if index < 8 else [(0,)]
-                    for part in parts:
-                        copy = pltpu.make_async_copy(
-                            params[index].at[part],
-                            local[index].at[part],
-                            sems.at[sum(map(len, copies.values()))],
-                        )
+                items = [
+                    (index, part)
+                    for index in range(8)
+                    for part in pieces_of(index, params[index].shape)
+                ]
+                early = [(index, (0,)) for index in range(8, held)]
+                for number, (index, part) in enumerate(early + items):
+                    copy = pltpu.make_async_copy(
+                        params[index].at[part], local[index].at[part], sems.at[number]
+                    )
+                    copies.setdefault(index, []).append(copy)
+                queue = [copy for index in range(8) for copy in copies[index]]
+                sizes = [
+                    2 * math.prod(params[index].shape) // len(copies[index])
+                    for index in range(8)
+                    for _ in copies[index]
+                ]
+                flight = {}
+
+                def launch():
+                    while queue and sum(flight.values()) < WINDOW:
+                        copy = queue.pop(0)
                         copy.start()
-                        copies.setdefault(index, []).append(copy)
+                        flight[id(copy)] = sizes.pop(0)
+
+                for index in range(8, held):
+                    copies[index][0].start()
+                launch()
                 for i, piece in enumerate(pieces if count > 1 else []):
                     begin = pl.multiple_of(places(i) * piece.shape[0], piece.shape[0])
                     assembled[pl.ds(begin, piece.shape[0]), :] = piece[...]
-                for index in range(8, held):
-                    copies[index][0].wait()
+                copies[8][0].wait()
 
             def wait(index, column=0):
                 if first and column // COLS < len(copies[index]):
-                    copies[index][column // COLS].wait()
+                    copy = copies[index][column // COLS]
+                    copy.wait()
+                    flight.pop(id(copy))
+                    launch()
 
             weights = local[:8]
             (up, down, query, key, value, out, expand, shrink) = weights
@@ -132,6 +151,10 @@
                 wait(DOWN, j)
                 part = dot(inner_s[...], down[0, :, j : j + cols])
                 start_s[:, j : j + cols] = inputs[:, j : j + cols].astype(F32) + 0.5 * part
+
+            if first:
+                for index in range(9, held):
+                    copies[index][0].wait()
 
             def attn_norm(at):
                 norm_s[at, :] = normalize(start_s[at, :], gains[1][...]).astype(BF16)

time: 165 us -> 163 us (0.988)
  no operation moved by 1% of the time
where the time goes in v5:
time: 163 us
  waiting for transfers between devices  118 us (72%)
  Pallas kernels  25.3 us (16%)
  starting transfers between devices  16.1 us (10%)
  local copies, waits for them, and re-layouts  2.91 us (2%)
    ppermute x7, waiting for transfers between devices, tick(): pieces = [lax.ppermute(kept, 'section', pairs)]  109 us
    pallas_call x8, Pallas kernels, block(): pl.pallas_call(block_kernel(heads, count, held, utterance_of, first, plac...  16.8 us
    ppermute x7, starting transfers between devices, tick(): pieces = [lax.ppermute(kept, 'section', pairs)]  9.04 us
    pallas_call x7, Pallas kernels, prefetch(): pl.pallas_call(run, out_shape=[pltpu.VMEM(p.shape, p.dtype) for p in para...  8.58 us
    all_to_all x1, waiting for transfers between devices, body(): own = lax.all_to_all(frames, 'tm', 0, 0, tiled=True)  6.19 us
    ppermute x3, starting transfers between devices, body(): lax.ppermute(rows_of((group_index + r) % peers), 'tm', [(j, (j + r) % pee...  3.61 us
    all_to_all x1, starting transfers between devices, body(): own = lax.all_to_all(frames, 'tm', 0, 0, tiled=True)  3.47 us
  transfers between devices with their start and end apart: 11, of which 10 were waited for; matrix products, arithmetic and copies ran while one was open for 1% of the time, Pallas kernels for 5%

profile of v5, /device:TPU:25, one launch (start us, length us, event | category | flops | bytes accessed | tf_op | source)
XLA Modules:
  0.0 162.8 jit_solution(16317721022324274597)
XLA Ops:
  0.0 3.5 %all-to-all-start = ((bf16[4,64,1024]{2,1,0:T(8,128)(2,1)}), bf16[4,64,1024]{2,1,0:T(8,128)(2,1)S(1)}, u32[]{:S(2)}, u32[]{:S(2)}) async-start(bf16[4,64,1024]{2,1,0:T(8,128)(2,1)} %param.19), calls=%async_computation | async-start | bytes 1048576 | tf_op jit(solution)/shard_map/all_to_all | solution.py:386
  4.5 6.2 %all-to-all-done = bf16[4,64,1024]{2,1,0:T(8,128)(2,1)S(1)} async-done(((bf16[4,64,1024]{2,1,0:T(8,128)(2,1)}), bf16[4,64,1024]{2,1,0:T(8,128)(2,1)S(1)}, u32[]{:S(2)}, u32[]{:S(2)}) %all-to-all-start) | async-done | bytes 524320 | tf_op jit(solution)/shard_map/all_to_all | solution.py:386
  10.8 1.2 block.6
  12.4 142.8 %while.13 = (s32[]{:T(128)}, bf16[256,1024]{1,0:T(8,128)(2,1)S(1)}, bf16[1,1024,2048]{2,1,0:T(8,128)(2,1)}, bf16[1,2048,1024]{2,1,0:T(8,128)(2,1)}, bf16[1,1024,...) while((s32[]{:T(128)}, bf16[256,1024]{1,0:T(8,128)(2,1)S(1)}, ...), condition=%wide.region_1.2_spmd, body=%wide.region_0.1_spmd.sunk | while | flops 2 | bytes 2097365 | solution.py:403
  12.4 1.3 collective-permute-start
  13.9 3.5 %collective-permute-done.refs_2_ = bf16[256,1024]{1,0:T(8,128)(2,1)S(1)} collective-permute-done((bf16[256,1024]{1,0:T(8,128)(2,1)S(1)}, bf16[256,1024]{1,0:T(8,128)(2,1)S(1)}, u32[]{:S(2)}, u32[]{:S(2)}) %collective-permute-start) | collective-permute-done | bytes 524320 | tf_op jit(solution)/shard_map/while/body/eval_jaxpr/ppermute | solution.py:399
  18.0 1.3 collective-permute-start
  19.5 9.0 %collective-permute-done.refs_2_ = bf16[256,1024]{1,0:T(8,128)(2,1)S(1)} collective-permute-done((bf16[256,1024]{1,0:T(8,128)(2,1)S(1)}, bf16[256,1024]{1,0:T(8,128)(2,1)S(1)}, u32[]{:S(2)}, u32[]{:S(2)}) %collective-permute-start) | collective-permute-done | bytes 524320 | tf_op jit(solution)/shard_map/while/body/eval_jaxpr/ppermute | solution.py:399
  29.1 1.3 collective-permute-start
  30.6 9.0 %collective-permute-done.refs_2_ = bf16[256,1024]{1,0:T(8,128)(2,1)S(1)} collective-permute-done((bf16[256,1024]{1,0:T(8,128)(2,1)S(1)}, bf16[256,1024]{1,0:T(8,128)(2,1)S(1)}, u32[]{:S(2)}, u32[]{:S(2)}) %collective-permute-start) | collective-permute-done | bytes 524320 | tf_op jit(solution)/shard_map/while/body/eval_jaxpr/ppermute | solution.py:399
  40.1 1.3 collective-permute-start
  41.7 9.0 %collective-permute-done.refs_2_ = bf16[256,1024]{1,0:T(8,128)(2,1)S(1)} collective-permute-done((bf16[256,1024]{1,0:T(8,128)(2,1)S(1)}, bf16[256,1024]{1,0:T(8,128)(2,1)S(1)}, u32[]{:S(2)}, u32[]{:S(2)}) %collective-permute-start) | collective-permute-done | bytes 524320 | tf_op jit(solution)/shard_map/while/body/eval_jaxpr/ppermute | solution.py:399
  51.2 1.3 collective-permute-start
  52.7 9.0 %collective-permute-done.refs_2_ = bf16[256,1024]{1,0:T(8,128)(2,1)S(1)} collective-permute-done((bf16[256,1024]{1,0:T(8,128)(2,1)S(1)}, bf16[256,1024]{1,0:T(8,128)(2,1)S(1)}, u32[]{:S(2)}, u32[]{:S(2)}) %collective-permute-start) | collective-permute-done | bytes 524320 | tf_op jit(solution)/shard_map/while/body/eval_jaxpr/ppermute | solution.py:399
  62.3 1.3 collective-permute-start
  63.8 9.0 %collective-permute-done.refs_2_ = bf16[256,1024]{1,0:T(8,128)(2,1)S(1)} collective-permute-done((bf16[256,1024]{1,0:T(8,128)(2,1)S(1)}, bf16[256,1024]{1,0:T(8,128)(2,1)S(1)}, u32[]{:S(2)}, u32[]{:S(2)}) %collective-permute-start) | collective-permute-done | bytes 524320 | tf_op jit(solution)/shard_map/while/body/eval_jaxpr/ppermute | solution.py:399
  73.4 1.3 collective-permute-start
  74.7 7.3 %prefetch.5 = (bf16[1,1024,2048]{2,1,0:T(8,128)(2,1)S(1)}, bf16[1,2048,1024]{2,1,0:T(8,128)(2,1)S(1)}, bf16[1,1024,1024]{2,1,0:T(8,128)(2,1)S(1)}, bf16[1,1024,1...) custom-call(s32[1]{0:T(128)} %bitcast.11.step.refs_0_, ...), custom_call_target="tpu_custom_call" | custom-call | tf_op jit(solution)/shard_map/while/body/eval_jaxpr/prefetch/pallas_call | solution.py:322
  82.0 60.8 %collective-permute-done.refs_2_ = bf16[256,1024]{1,0:T(8,128)(2,1)S(1)} collective-permute-done((bf16[256,1024]{1,0:T(8,128)(2,1)S(1)}, bf16[256,1024]{1,0:T(8,128)(2,1)S(1)}, u32[]{:S(2)}, u32[]{:S(2)}) %collective-permute-start) | collective-permute-done | bytes 524320 | tf_op jit(solution)/shard_map/while/body/eval_jaxpr/ppermute | solution.py:399
  142.8 12.3 %block.7 = bf16[256,1024]{1,0:T(8,128)(2,1)S(1)} custom-call(s32[1]{0:T(128)} %bitcast.11.step.refs_0_, s32[4]{0:T(128)S(1)} %get-tuple-element.526.refs_1_, bf16[256,1024]{1,0:T(8,128)(2,1)S(1)} %collective-permute-done.refs_2_, bf16[1,1024,2048]{2,1,0:T(8,128)(2,1)S(1)} %get-tuple-element.456.refs_3_, ...), custom_call_target="tpu_custom_call", output_to_operand_aliasing={{}: (18, {})} | custom-call | tf_op jit(solution)/shard_map/while/body/eval_jaxpr/block/pallas_call | solution.py:288
  155.2 1.2 collective-permute-start.1
  156.6 2.1 %collective-permute-start.3 = (bf16[64,1024]{1,0:T(8,128)(2,1)S(1)}, bf16[64,1024]{1,0:T(8,128)(2,1)S(1)}, u32[]{:S(2)}, u32[]{:S(2)}) collective-permute-start(bf16[64,1024]{1,0:T(8,128)(2,1)S(1)} %get-tuple-element.329), channel_id=1, source_target_pairs={{0,3},{1,0},{2,1},{3,2},{4,7},{5,4},{6,5},{7,6},{8,11},{9,8},{10,9... | collective-permute-start | bytes 393224 | tf_op jit(solution)/shard_map/ppermute | solution.py:412
  158.9 1.2 collective-permute-done.1
  160.0 1.3 collective-permute-done.2
  (40 shorter events, 7.8 us)
Async XLA Ops:
  0.0 10.7 %all-to-all-start = ((bf16[4,64,1024]{2,1,0:T(8,128)(2,1)}), bf16[4,64,1024]{2,1,0:T(8,128)(2,1)S(1)}, u32[]{:S(2)}, u32[]{:S(2)}) async-start(bf16[4,64,1024]{2,1,0:T(8,128)(2,1)} %param.19), calls=%async_computation | async-start | bytes 1048576 | tf_op jit(solution)/shard_map/all_to_all | solution.py:386
  10.7 1.6 copy-start
  10.7 1.6 copy-start.2
  10.7 1.6 copy-start.3
  10.7 1.6 copy-start.4
  10.8 1.6 copy-start.5
  10.8 1.6 copy-start.6
  10.8 1.5 copy-start.7
  10.8 1.5 copy-start.8
  12.4 5.1 %collective-permute-start = (bf16[256,1024]{1,0:T(8,128)(2,1)S(1)}, bf16[256,1024]{1,0:T(8,128)(2,1)S(1)}, u32[]{:S(2)}, u32[]{:S(2)}) collective-permute-start(bf16[256,1024]{1,0:T(8,128)(2,1)S(1)} %get-tuple-element.491.refs_18_), channel_id=1, source_target_pairs={{0,4},{4,8},{8,12},{12,16},{16,20},{20,24},{24,28},{1,5},{5,9},{9,... | collective-permute-start | bytes 1572872 | tf_op jit(solution)/shard_map/while/body/eval_jaxpr/ppermute | solution.py:399
  18.0 10.5 %collective-permute-start = (bf16[256,1024]{1,0:T(8,128)(2,1)S(1)}, bf16[256,1024]{1,0:T(8,128)(2,1)S(1)}, u32[]{:S(2)}, u32[]{:S(2)}) collective-permute-start(bf16[256,1024]{1,0:T(8,128)(2,1)S(1)} %get-tuple-element.491.refs_18_), channel_id=1, source_target_pairs={{0,4},{4,8},{8,12},{12,16},{16,20},{20,24},{24,28},{1,5},{5,9},{9,... | collective-permute-start | bytes 1572872 | tf_op jit(solution)/shard_map/while/body/eval_jaxpr/ppermute | solution.py:399
  29.1 10.5 %collective-permute-start = (bf16[256,1024]{1,0:T(8,128)(2,1)S(1)}, bf16[256,1024]{1,0:T(8,128)(2,1)S(1)}, u32[]{:S(2)}, u32[]{:S(2)}) collective-permute-start(bf16[256,1024]{1,0:T(8,128)(2,1)S(1)} %get-tuple-element.491.refs_18_), channel_id=1, source_target_pairs={{0,4},{4,8},{8,12},{12,16},{16,20},{20,24},{24,28},{1,5},{5,9},{9,... | collective-permute-start | bytes 1572872 | tf_op jit(solution)/shard_map/while/body/eval_jaxpr/ppermute | solution.py:399
  40.1 10.5 %collective-permute-start = (bf16[256,1024]{1,0:T(8,128)(2,1)S(1)}, bf16[256,1024]{1,0:T(8,128)(2,1)S(1)}, u32[]{:S(2)}, u32[]{:S(2)}) collective-permute-start(bf16[256,1024]{1,0:T(8,128)(2,1)S(1)} %get-tuple-element.491.refs_18_), channel_id=1, source_target_pairs={{0,4},{4,8},{8,12},{12,16},{16,20},{20,24},{24,28},{1,5},{5,9},{9,... | collective-permute-start | bytes 1572872 | tf_op jit(solution)/shard_map/while/body/eval_jaxpr/ppermute | solution.py:399
  51.2 10.5 %collective-permute-start = (bf16[256,1024]{1,0:T(8,128)(2,1)S(1)}, bf16[256,1024]{1,0:T(8,128)(2,1)S(1)}, u32[]{:S(2)}, u32[]{:S(2)}) collective-permute-start(bf16[256,1024]{1,0:T(8,128)(2,1)S(1)} %get-tuple-element.491.refs_18_), channel_id=1, source_target_pairs={{0,4},{4,8},{8,12},{12,16},{16,20},{20,24},{24,28},{1,5},{5,9},{9,... | collective-permute-start | bytes 1572872 | tf_op jit(solution)/shard_map/while/body/eval_jaxpr/ppermute | solution.py:399
  62.3 10.5 %collective-permute-start = (bf16[256,1024]{1,0:T(8,128)(2,1)S(1)}, bf16[256,1024]{1,0:T(8,128)(2,1)S(1)}, u32[]{:S(2)}, u32[]{:S(2)}) collective-permute-start(bf16[256,1024]{1,0:T(8,128)(2,1)S(1)} %get-tuple-element.491.refs_18_), channel_id=1, source_target_pairs={{0,4},{4,8},{8,12},{12,16},{16,20},{20,24},{24,28},{1,5},{5,9},{9,... | collective-permute-start | bytes 1572872 | tf_op jit(solution)/shard_map/while/body/eval_jaxpr/ppermute | solution.py:399
  73.4 69.5 %collective-permute-start = (bf16[256,1024]{1,0:T(8,128)(2,1)S(1)}, bf16[256,1024]{1,0:T(8,128)(2,1)S(1)}, u32[]{:S(2)}, u32[]{:S(2)}) collective-permute-start(bf16[256,1024]{1,0:T(8,128)(2,1)S(1)} %get-tuple-element.491.refs_18_), channel_id=1, source_target_pairs={{0,4},{4,8},{8,12},{12,16},{16,20},{20,24},{24,28},{1,5},{5,9},{9,... | collective-permute-start | bytes 1572872 | tf_op jit(solution)/shard_map/while/body/eval_jaxpr/ppermute | solution.py:399
  155.2 4.9 %collective-permute-start.1 = (bf16[64,1024]{1,0:T(8,128)(2,1)S(1)}, bf16[64,1024]{1,0:T(8,128)(2,1)S(1)}, u32[]{:S(2)}, u32[]{:S(2)}) collective-permute-start(bf16[64,1024]{1,0:T(8,128)(2,1)S(1)} %get-tuple-element.331), channel_id=1, source_target_pairs={{0,1},{1,2},{2,3},{3,0},{4,5},{5,6},{6,7},{7,4},{8,9},{9,10},{10,1... | collective-permute-start | bytes 393224 | tf_op jit(solution)/shard_map/ppermute | solution.py:412
  156.4 5.0 %collective-permute-start.2 = (bf16[64,1024]{1,0:T(8,128)(2,1)S(1)}, bf16[64,1024]{1,0:T(8,128)(2,1)S(1)}, u32[]{:S(2)}, u32[]{:S(2)}) collective-permute-start(bf16[64,1024]{1,0:T(8,128)(2,1)S(1)} %get-tuple-element.330), channel_id=1, source_target_pairs={{0,2},{1,3},{2,0},{3,1},{4,6},{5,7},{6,4},{7,5},{8,10},{9,11},{10,... | collective-permute-start | bytes 393224 | tf_op jit(solution)/shard_map/ppermute | solution.py:412
  156.6 4.8 %collective-permute-start.3 = (bf16[64,1024]{1,0:T(8,128)(2,1)S(1)}, bf16[64,1024]{1,0:T(8,128)(2,1)S(1)}, u32[]{:S(2)}, u32[]{:S(2)}) collective-permute-start(bf16[64,1024]{1,0:T(8,128)(2,1)S(1)} %get-tuple-element.329), channel_id=1, source_target_pairs={{0,3},{1,0},{2,1},{3,2},{4,7},{5,4},{6,5},{7,6},{8,11},{9,8},{10,9... | collective-permute-start | bytes 393224 | tf_op jit(solution)/shard_map/ppermute | solution.py:412
  161.3 0.8 copy-start.1
